TPU v7x, 512 devices: a 4x2x32 block of a 4x16x32 slice. The times are simulated.
512 devices in a mesh: grp: 2 (over y), pulse: 32 (over z), chan: 4 (over x), sub: 2 (over core).
Axes of the slice: x: 4, y: 2, z: 32, core: 2. Of those that a mesh axis runs over, the one named last changes fastest.
The devices are a block of a 4x16x32 slice.
Arguments:
- samples: int32 [2, 32, 512, 4096], P(None, ('grp', 'chan', 'sub'), 'pulse'), parts along dimension 1, may hold values from -2048 to 2047
- replica: float32 [2, 4096], replicated, may hold values from -6 to 6
- window: int32 [32, 2], P(('grp', 'chan', 'sub')), parts along dimension 0, may hold values from 1 to 28, as said below
- thresh: int32 [32, 2], P(('grp', 'chan', 'sub')), parts along dimension 0, may hold values from 2 to 32, as said below
Outputs:
- ratio_map: float32 [32, 512, 4096], P(('grp', 'chan', 'sub'), None, 'pulse'), parts along dimension 0
- detections: float32 [2], P('grp'), parts along dimension 0
There are 2 independent parts, one for each index of `grp`. A program takes and returns all parts, laid end to end along the dimension named above; an argument that names none is the same for every part. Nothing has to cross between parts.
Inputs may be any that keep to these rules, and one draw needn't show every extreme that they name: `window`: column 0 is a channel's guard gates on each side, 1 to 4; column 1 its training gates on each side, 14 to 28; some channel has both at their most. `thresh`: column 0 is a numerator of 8 to 32, column 1 a denominator of 2 to 4.
All inputs are finite; a program needn't handle non-finite values.
Results may differ from a plain program's by a relative error of at most 0.0003.
Values sent between devices are 32-bit elements; how exact they have to be, the bound alone decides.
No kernel may reach another device: no remote copies, remote signals or barrier semaphores. Data moves between devices by JAX's collectives and lax.ppermute only.
A program may use at most 64 MiB of HBM per device.

v0:
```python
import functools
import math

import jax
import jax.numpy as jnp
import numpy as np
from jax import lax
from jax.experimental import pallas as pl
from jax.experimental.pallas import tpu as pltpu
from jax.sharding import PartitionSpec as P

PULSES = 512
RANGE = 4096
GUARD_MAX = 4
TRAIN_MAX = 28

EPSILON = 1e-06
INPUT_SCALE = 1.0 / 2048.0
MARGIN = GUARD_MAX + TRAIN_MAX

LANES = 128
ROWS = 8
FAN = 32
TAIL = RANGE // FAN
FINE = PULSES // FAN
PARTS = MARGIN
PACK = LANES // PARTS
F32 = jnp.float32
BF16 = jnp.bfloat16
MEBI = 1 << 20
ORDER = [place ^ (place >> 1) for place in range(FAN)]


def slot(device):
    return ORDER.index(device)


def split_table(table):
    high = table.astype(BF16)
    low = (table - high.astype(np.float64)).astype(BF16)
    return np.stack([high, low])


def unit(product, period):
    angle = 2.0 * np.pi / period * (np.asarray(product, np.int64) % period)
    return np.cos(angle), np.sin(angle)


def range_tables():
    b = np.arange(TAIL)[:, None]
    col = np.arange(TAIL)[None, :]
    freq = 4 * (col % FAN) + col // FAN
    cos, sin = unit(b * freq, TAIL)
    forward = np.block([[cos, -sin], [sin, cos]])
    inverse = forward.T
    k1 = np.arange(FAN)[:, None]
    cos, sin = unit(k1 * np.arange(TAIL)[None, :], RANGE)
    twiddle = np.stack([cos, sin]).astype(np.float32)
    return split_table(forward), split_table(inverse), twiddle


def doppler_tables():
    tiles = []
    for t in range(FAN // ROWS):
        table = np.zeros((2, FINE, ROWS, ROWS, 2, FINE))
        for d1 in range(ROWS):
            bins = 8 * t + d1 + FAN * np.arange(FINE)[:, None]
            cos, sin = unit(bins * np.arange(FINE)[None, :], PULSES)
            table[0, :, d1, d1, 0] = cos
            table[0, :, d1, d1, 1] = sin
            table[1, :, d1, d1, 0] = -sin
            table[1, :, d1, d1, 1] = cos
        tiles.append(split_table(table.reshape(2 * PULSES // 4, 2 * PULSES // 4)))
    return np.stack(tiles)


def add(x, y):
    return (x[0] + y[0], x[1] + y[1])


def sub(x, y):
    return (x[0] - y[0], x[1] - y[1])


def turn(x, sign):
    return (-x[1], x[0]) if sign > 0 else (x[1], -x[0])


def add_turn(x, y, sign):
    if sign > 0:
        return (x[0] - y[1], x[1] + y[0])
    return (x[0] + y[1], x[1] - y[0])


def by_constant(x, index, period, sign):
    index = index % period
    if index == 0:
        return x
    angle = 2.0 * math.pi * index / period
    cos, sin = math.cos(angle), sign * math.sin(angle)
    if 8 * index == period:
        return ((x[0] - x[1]) * cos, (x[0] + x[1]) * cos) if sign > 0 else ((x[0] + x[1]) * cos, (x[1] - x[0]) * cos)
    if 4 * index == period:
        return turn(x, sign)
    return (x[0] * cos - x[1] * sin, x[0] * sin + x[1] * cos)


def fft4(x, sign):
    a, b = add(x[0], x[2]), sub(x[0], x[2])
    c, d = add(x[1], x[3]), sub(x[1], x[3])
    return [add(a, c), add_turn(b, d, sign), sub(a, c), add_turn(b, d, -sign)]


def fft8(x, sign):
    even, odd = fft4(x[0::2], sign), fft4(x[1::2], sign)
    root = math.sqrt(0.5)
    out = [None] * 8
    out[0], out[4] = add(even[0], odd[0]), sub(even[0], odd[0])
    out[2], out[6] = add_turn(even[2], odd[2], sign), add_turn(even[2], odd[2], -sign)
    for k in (1, 3):
        o = odd[k]
        if k == 1:
            w = (o[0] - o[1], o[0] + o[1]) if sign > 0 else (o[0] + o[1], o[1] - o[0])
        else:
            w = (-o[0] - o[1], o[0] - o[1]) if sign > 0 else (o[1] - o[0], -o[0] - o[1])
        w = (w[0] * root, w[1] * root)
        out[k], out[k + 4] = add(even[k], w), sub(even[k], w)
    return out


def fft32(load, keep, fetch, store, sign):
    for n2 in range(8):
        mid = fft4([load(n2 + 8 * n1) for n1 in range(4)], sign)
        for k1 in range(4):
            keep(k1 * 8 + n2, by_constant(mid[k1], n2 * k1, 32, sign))
    for k1 in range(4):
        out = fft8([fetch(k1 * 8 + n2) for n2 in range(8)], sign)
        for k2 in range(8):
            store(k1 + 4 * k2, out[k2])


def split(x):
    high = x.astype(BF16)
    return high, (x - high.astype(F32)).astype(BF16)


def dot(x, y):
    return jnp.dot(x, y, preferred_element_type=F32)


def compress_kernel(
    x_hbm, rep_hbm, fwd_hbm, inv_hbm, twd_hbm, o_ref,
    x_ref, rep_ref, fwd_ref, inv_ref, twd_ref, h_ref, mid_ref, high_ref, low_ref, sems,
):
    channels, pulses = x_hbm.shape[1], x_hbm.shape[2]
    sets = [(c, p) for c in range(channels) for p in range(0, pulses, ROWS)]
    loads = [
        pltpu.make_async_copy(x_hbm.at[:, c, pl.ds(p, ROWS)], x_ref.at[i], sems.at[i]) for i, (c, p) in enumerate(sets)
    ]
    n = len(sets)
    load_rep = pltpu.make_async_copy(rep_hbm, rep_ref, sems.at[n])
    load_twd = pltpu.make_async_copy(twd_hbm, twd_ref, sems.at[n + 1])
    load_fwd = pltpu.make_async_copy(fwd_hbm, fwd_ref, sems.at[n + 2])
    load_inv = pltpu.make_async_copy(inv_hbm, inv_ref, sems.at[n + 3])
    for load in [loads[0], load_rep, load_twd, load_fwd, *loads[1:], load_inv]:
        load.start()

    load_rep.wait()
    for part in range(2):
        turned = rep_ref[pl.ds(part, FAN, stride=2), :].T
        h_ref[part] = jnp.concatenate([turned[q * FAN : (q + 1) * FAN] for q in range(4)], axis=1)
    load_twd.wait()

    def row(ref, part, k):
        return jnp.broadcast_to(ref[part, k : k + 1, :], (ROWS, LANES))

    def put(i, k, value):
        for part in range(2):
            high, low = split(value[part])
            high_ref[i, k * ROWS : (k + 1) * ROWS, part * LANES : (part + 1) * LANES] = high
            low_ref[i, k * ROWS : (k + 1) * ROWS, part * LANES : (part + 1) * LANES] = low

    def product(i, table):
        high = high_ref[i]
        return dot(high, table[0]) + dot(low_ref[i], table[0]) + dot(high, table[1])

    for i, (c, p) in enumerate(sets):
        loads[i].wait()

        def load(a, i=i):
            return tuple(x_ref[i, part, :, a * LANES : (a + 1) * LANES].astype(F32) for part in range(2))

        def keep(j, value, i=i):
            mid_ref[i, 0, j], mid_ref[i, 1, j] = value

        def fetch(j, i=i):
            return (mid_ref[i, 0, j], mid_ref[i, 1, j])

        def twisted(k, value, i=i):
            cos, sin = row(twd_ref, 0, k) , row(twd_ref, 1, k)
            put(i, k, (value[0] * cos + value[1] * sin, value[1] * cos - value[0] * sin))

        fft32(load, keep, fetch, twisted, -1)
        if i == 0:
            load_fwd.wait()
        spectrum = product(i, fwd_ref)
        for k in range(FAN):
            re = spectrum[k * ROWS : (k + 1) * ROWS, :LANES]
            im = spectrum[k * ROWS : (k + 1) * ROWS, LANES:]
            h_re, h_im = row(h_ref, 0, k), row(h_ref, 1, k)
            put(i, k, (re * h_re - im * h_im, re * h_im + im * h_re))
        if i == 0:
            load_inv.wait()
        back = product(i, inv_ref)

        def untwisted(k, back=back):
            re = back[k * ROWS : (k + 1) * ROWS, :LANES]
            im = back[k * ROWS : (k + 1) * ROWS, LANES:]
            cos, sin = row(twd_ref, 0, k), row(twd_ref, 1, k)
            return (re * cos - im * sin, im * cos + re * sin)

        def store(a, value, i=i):
            for part in range(2):
                o_ref[slot(a), i * 2 * ROWS + part * ROWS : i * 2 * ROWS + (part + 1) * ROWS, :] = value[part]

        fft32(untwisted, keep, fetch, store, 1)


def compress(samples, replica, limit):
    fwd, inv, twd = [jnp.asarray(table) for table in range_tables()]
    sets = samples.shape[1] * samples.shape[2] // ROWS
    rep = replica.reshape(2, FAN, LANES).transpose(1, 0, 2).reshape(2 * FAN, LANES)
    any_space = pl.BlockSpec(memory_space=pltpu.HBM)
    return pl.pallas_call(
        compress_kernel,
        out_shape=pltpu.VMEM((FAN, sets * 2 * ROWS, LANES), F32),
        in_specs=[any_space] * 5,
        out_specs=pl.BlockSpec(memory_space=pltpu.VMEM),
        scratch_shapes=[
            pltpu.VMEM((sets, 2, ROWS, RANGE), jnp.int32),
            pltpu.VMEM((2 * FAN, LANES), F32),
            pltpu.VMEM((2, 2 * TAIL, 2 * TAIL), BF16),
            pltpu.VMEM((2, 2 * TAIL, 2 * TAIL), BF16),
            pltpu.VMEM((2, FAN, LANES), F32),
            pltpu.VMEM((2, FAN, LANES), F32),
            pltpu.VMEM((sets, 2, FAN, ROWS, LANES), F32),
            pltpu.VMEM((sets, FAN * ROWS, 2 * LANES), BF16),
            pltpu.VMEM((sets, FAN * ROWS, 2 * LANES), BF16),
            pltpu.SemaphoreType.DMA((sets + 4,)),
        ],
        compiler_params=pltpu.CompilerParams(vmem_limit_bytes=limit),
        cost_estimate=pl.CostEstimate(flops=2 * 10**9, bytes_accessed=2 * MEBI, transcendentals=0),
        name="compress",
    )(*[pltpu.with_memory_space_constraint(x, pltpu.HBM) for x in (samples, rep, fwd, inv, twd)])


def doppler_kernel(x_ref, tab_ref, pow_ref, low_edge_ref, high_edge_ref, mid_ref, part_ref):
    channels = pow_ref.shape[0]
    sets = x_ref.shape[1] // (2 * ROWS)
    halves = sets // channels
    for i in range(sets):
        c, half = i // halves, i % halves

        def load(s, i=i):
            return tuple(x_ref[slot(s), i * 2 * ROWS + part * ROWS : i * 2 * ROWS + (part + 1) * ROWS, :] for part in range(2))

        def keep(j, value, i=i):
            mid_ref[i, 0, j], mid_ref[i, 1, j] = value

        def fetch(j, i=i):
            return (mid_ref[i, 0, j], mid_ref[i, 1, j])

        def store(k, value, c=c, half=half):
            tile, d1 = k // ROWS, k % ROWS
            for part in range(2):
                at = (d1 * 2 + part) * FINE + half * ROWS
                part_ref[tile, at : at + ROWS, c * LANES : (c + 1) * LANES] = value[part]

        fft32(load, keep, fetch, store, -1)
    scale = INPUT_SCALE * INPUT_SCALE / (float(RANGE) * float(RANGE) * PULSES)
    for tile in range(FAN // ROWS):
        high, low = split(part_ref[tile])
        out = dot(tab_ref[tile, 0], high) + dot(tab_ref[tile, 0], low) + dot(tab_ref[tile, 1], high)
        half = out.shape[0] // 2
        power = (out[:half] * out[:half] + out[half:] * out[half:]) * scale
        for d2 in range(FINE):
            for c in range(channels):
                at = d2 * FAN + tile * ROWS
                pow_ref[c, at : at + ROWS, :] = power[d2 * ROWS : (d2 + 1) * ROWS, c * LANES : (c + 1) * LANES]
    rows = PULSES // PACK
    lane = lax.broadcasted_iota(jnp.int32, (rows, LANES), 1)
    for c in range(channels):
        low_piece = high_piece = None
        for b in range(PACK):
            x = pow_ref[c, b * rows : (b + 1) * rows, :]
            low = pltpu.roll(x, b * PARTS, 1) if b else x
            shift = (b * PARTS - (LANES - PARTS)) % LANES
            high = pltpu.roll(x, shift, 1) if shift else x
            mine = lane >= b * PARTS
            low_piece = low if low_piece is None else jnp.where(mine, low, low_piece)
            high_piece = high if high_piece is None else jnp.where(mine, high, high_piece)
        low_edge_ref[c * rows : (c + 1) * rows, :] = low_piece
        high_edge_ref[c * rows : (c + 1) * rows, :] = high_piece


def doppler(received, channels, limit):
    sets = received.shape[1] // (2 * ROWS)
    vmem = pl.BlockSpec(memory_space=pltpu.VMEM)
    edge = pltpu.VMEM((channels * PULSES // PACK, LANES), F32)
    tables = jnp.asarray(doppler_tables())
    return pl.pallas_call(
        doppler_kernel,
        out_shape=(pltpu.VMEM((channels, PULSES, LANES), F32), edge, edge),
        in_specs=[vmem, vmem],
        out_specs=(vmem, vmem, vmem),
        scratch_shapes=[
            pltpu.VMEM((sets, 2, FAN, ROWS, LANES), F32),
            pltpu.VMEM((FAN // ROWS, 2 * FINE * ROWS, channels * LANES), F32),
        ],
        compiler_params=pltpu.CompilerParams(vmem_limit_bytes=limit),
        cost_estimate=pl.CostEstimate(flops=2 * 10**9, bytes_accessed=2 * MEBI, transcendentals=0),
        name="doppler",
    )(
        pltpu.with_memory_space_constraint(received, pltpu.VMEM),
        pltpu.with_memory_space_constraint(tables, pltpu.VMEM),
    )


def windows_kernel(groups, window_ref, thresh_ref, place_ref, core_ref, side_ref, line_ref):
    channels = window_ref.shape[0]
    total = groups * LANES
    gate = lax.broadcasted_iota(jnp.int32, (ROWS, LANES), 1) + place_ref[0] * LANES
    row_id = lax.broadcasted_iota(jnp.int32, (LANES, LANES), 0)
    col_id = lax.broadcasted_iota(jnp.int32, (LANES, LANES), 1)
    piece, inner = row_id // PARTS, row_id % PARTS
    core_ref[...] = jnp.zeros_like(core_ref)
    for c in range(channels):
        guard, train = window_ref[c, 0], window_ref[c, 1]
        reach = guard + train

        def band(offset, extra=True):
            distance = jnp.abs(offset)
            return jnp.where((distance > guard) & (distance <= reach) & extra, 1.0, 0.0).astype(BF16)

        core_ref[c * LANES : (c + 1) * LANES, c * LANES : (c + 1) * LANES] = band(row_id - col_id)
        for b in range(PACK):
            at = b * LANES
            side_ref[c, :LANES, at : at + LANES] = band(inner - PARTS - col_id, piece == b)
            side_ref[c, LANES:, at : at + LANES] = band(inner + LANES - col_id, piece == b)
        ahead = total - 1 - gate
        cells = jnp.minimum(gate, reach) - jnp.minimum(gate, guard)
        cells = cells + jnp.minimum(ahead, reach) - jnp.minimum(ahead, guard)
        line_ref[c, 0] = cells.astype(F32)
        over = jnp.zeros((ROWS, LANES), F32) + thresh_ref[c, 1].astype(F32)
        line_ref[c, 1] = over / thresh_ref[c, 0].astype(F32)


def windows(window, thresh, place, groups, limit):
    channels = window.shape[0]
    vmem = pl.BlockSpec(memory_space=pltpu.VMEM)
    smem = pl.BlockSpec(memory_space=pltpu.SMEM)
    return pl.pallas_call(
        functools.partial(windows_kernel, groups),
        out_shape=(
            pltpu.VMEM((channels * LANES, channels * LANES), BF16),
            pltpu.VMEM((channels, 2 * LANES, PACK * LANES), BF16),
            pltpu.VMEM((channels, 2, ROWS, LANES), F32),
        ),
        in_specs=[smem, smem, smem],
        out_specs=(vmem, vmem, vmem),
        compiler_params=pltpu.CompilerParams(vmem_limit_bytes=limit),
        cost_estimate=pl.CostEstimate(flops=10**7, bytes_accessed=MEBI, transcendentals=0),
        name="windows",
    )(window, thresh, place)


def core_kernel(pow_ref, band_ref, noise_ref):
    channels = pow_ref.shape[0]
    high, low = split(jnp.concatenate([pow_ref[c] for c in range(channels)], axis=1))
    noise = dot(high, band_ref[...]) + dot(low, band_ref[...])
    for c in range(channels):
        noise_ref[c] = noise[:, c * LANES : (c + 1) * LANES]


def core(power, band, limit):
    vmem = pl.BlockSpec(memory_space=pltpu.VMEM)
    return pl.pallas_call(
        core_kernel,
        out_shape=pltpu.VMEM(power.shape, F32),
        in_specs=[vmem, vmem],
        out_specs=vmem,
        compiler_params=pltpu.CompilerParams(vmem_limit_bytes=limit),
        cost_estimate=pl.CostEstimate(flops=2 * 10**9, bytes_accessed=MEBI, transcendentals=0),
        name="core",
    )(in_vmem(power), in_vmem(band))


def in_vmem(x):
    return pltpu.with_memory_space_constraint(x, pltpu.VMEM)


def cfar_kernel(pow_ref, noise_ref, left_ref, right_ref, side_ref, line_ref, ratio_ref, soft_ref):
    channels = pow_ref.shape[0]
    rows = PULSES // PACK
    soft_sum = jnp.zeros((ROWS, LANES), F32)
    for c in range(channels):
        halo = jnp.concatenate([ref[c * rows : (c + 1) * rows, :] for ref in (left_ref, right_ref)], axis=1)
        high, low = split(halo)
        side = dot(high, side_ref[c]) + dot(low, side_ref[c])
        cells = jnp.concatenate([line_ref[c, 0]] * (rows // ROWS), axis=0)
        over = jnp.concatenate([line_ref[c, 1]] * (rows // ROWS), axis=0)
        for b in range(PACK):
            at = b * rows
            noise = noise_ref[c, at : at + rows, :] + side[:, b * LANES : (b + 1) * LANES]
            ratio = pow_ref[c, at : at + rows, :] * cells / (noise + EPSILON)
            ratio_ref[c, at : at + rows, :] = ratio
            soft = jnp.clip(ratio * over - 1.0, 0.0, 1.0)
            soft_sum = soft_sum + soft.reshape(rows // ROWS, ROWS, LANES).sum(axis=0)
    soft_ref[...] = jnp.broadcast_to(jnp.sum(soft_sum, axis=0, keepdims=True), soft_ref.shape)


def cfar(power, noise, left, right, side, line, peers, limit):
    vmem = pl.BlockSpec(memory_space=pltpu.VMEM)
    return pl.pallas_call(
        cfar_kernel,
        out_shape=(pltpu.VMEM(power.shape, F32), pltpu.VMEM((peers, LANES), F32)),
        in_specs=[vmem] * 6,
        out_specs=(vmem, vmem),
        compiler_params=pltpu.CompilerParams(vmem_limit_bytes=limit),
        cost_estimate=pl.CostEstimate(flops=10**9, bytes_accessed=2 * MEBI, transcendentals=0),
        name="cfar",
    )(*[in_vmem(x) for x in (power, noise, left, right, side, line)])


def local(samples, replica, window, thresh):
    groups = lax.axis_size("pulse")
    channels = samples.shape[1]
    assert samples.shape[3] == RANGE and groups == FAN and samples.shape[2] == FINE
    limit = 24 * MEBI
    ready = compress(samples, replica, limit)
    received = lax.all_to_all(ready, "pulse", 0, 0, axis_index_groups=[ORDER])
    place = lax.axis_index("pulse").reshape(1)
    band, side, line = windows(window, thresh, place, groups, limit)
    power, low_edge, high_edge = doppler(received, channels, limit)
    ends = groups - 1
    left = lax.ppermute(high_edge, "pulse", [(i, i + 1) for i in range(ends)])
    right = lax.ppermute(low_edge, "pulse", [(i + 1, i) for i in range(ends)])
    noise = core(power, band, limit)
    peers = lax.axis_size("chan") * lax.axis_size("sub")
    ratio_map, soft = cfar(power, noise, left, right, side, line, peers, limit)
    plane = jnp.sum(lax.all_to_all(soft.reshape(peers, 1, LANES), ("chan", "sub"), 0, 0), axis=0, keepdims=True)
    counts = lax.all_to_all(jnp.broadcast_to(plane, (groups, 1, LANES)), "pulse", 0, 0)
    detections = jnp.sum(counts) * (1024.0 / (PULSES * RANGE))
    return (ratio_map, detections.reshape(1))


def solution(mesh):
    in_specs = (
        P(None, ("grp", "chan", "sub"), "pulse", None),
        P(),
        P(("grp", "chan", "sub"), None),
        P(("grp", "chan", "sub"), None),
    )
    out_specs = (P(("grp", "chan", "sub"), None, "pulse"), P("grp"))
    return jax.shard_map(local, mesh=mesh, in_specs=in_specs, out_specs=out_specs, check_vma=False)
```

profile of v0, /device:TPU:40, one launch (start us, length us, event | category | flops | bytes accessed | tf_op | source)
XLA Modules:
  0.0 212.7 jit_solution(5641363562566314875)
XLA Ops:
  0.6 5.3 %compress.1 = f32[32,64,128]{2,1,0:T(8,128)} custom-call(s32[2,2,16,4096]{3,2,1,0:T(8,128)} %x_hbm.1, f32[64,128]{1,0:T(8,128)} %bitcast.13, bf16[2,256,256]{2,1,0:T(8,128)(2,1)} %constant.18.clone.fwd_hbm, bf16[2,256,256]{2,1,0:T(8,128)(2,1)} %constant.19.clone.inv_hbm, f32[2,32,128]{2,1,0:T(8,128)} %constant.20.clone.twd_hbm), custom_call_target="tpu_custom_call" | custom-call | flops 2000000000 | bytes 2097152 | tf_op jit(solution)/shard_map/compress/pallas_call | solution.py:234
  5.9 0.0 copy-start.1
  6.0 0.0 copy-start.2
  6.0 45.9 %all-to-all-start = ((f32[32,64,128]{2,1,0:T(8,128)}), f32[32,64,128]{2,1,0:T(8,128)S(1)}, u32[]{:S(2)}, u32[]{:S(2)}) async-start(f32[32,64,128]{2,1,0:T(8,128)} %compress.1), calls=%async_computation | async-start | bytes 2097152 | tf_op jit(solution)/shard_map/all_to_all | solution.py:441
  51.9 0.0 copy-start
  51.9 0.0 copy-done.1
  51.9 0.7 copy-done
  52.6 0.7 windows.1
  53.3 99.0 %all-to-all-done.x_ref = f32[32,64,128]{2,1,0:T(8,128)S(1)} async-done(((f32[32,64,128]{2,1,0:T(8,128)}), f32[32,64,128]{2,1,0:T(8,128)S(1)}, u32[]{:S(2)}, u32[]{:S(2)}) %all-to-all-start) | async-done | bytes 1048608 | tf_op jit(solution)/shard_map/all_to_all | solution.py:441
  152.3 0.0 copy-done.2
  152.3 1.0 doppler.1
  153.3 3.8 %collective-permute-start = (f32[256,128]{1,0:T(8,128)S(1)}, f32[256,128]{1,0:T(8,128)S(1)}, u32[]{:S(2)}, u32[]{:S(2)}) collective-permute-start(f32[256,128]{1,0:T(8,128)S(1)} %get-tuple-element.12), channel_id=1, source_target_pairs={{0,8},{8,16},{16,24},{24,32},{32,40},{40,48},{48,56},{56,64},{64,7... | collective-permute-start | bytes 393224 | tf_op jit(solution)/shard_map/ppermute | solution.py:446
  157.1 1.3 collective-permute-start.1
  158.4 0.3 core.1.noise_ref
  158.7 0.9 collective-permute-done.left_ref
  159.6 4.4 %collective-permute-done.1.right_ref = f32[256,128]{1,0:T(8,128)S(1)} collective-permute-done((f32[256,128]{1,0:T(8,128)S(1)}, f32[256,128]{1,0:T(8,128)S(1)}, u32[]{:S(2)}, u32[]{:S(2)}) %collective-permute-start.1) | collective-permute-done | bytes 131104 | tf_op jit(solution)/shard_map/ppermute | solution.py:447
  164.0 0.4 cfar.1
  164.4 9.7 %all_to_all.15 = f32[8,1,128]{2,1,0:T(1,128)S(1)} all-to-all(f32[8,1,128]{2,1,0:T(1,128)S(1)} %bitcast.11), channel_id=1, replica_groups=mesh['grp'=2,'pulse'=32,'chan'=4,'sub'=2] {'chan','sub'}, dimensions={0} | all-to-all | bytes 8192 | tf_op jit(solution)/shard_map/all_to_all | solution.py:451
  174.1 0.6 broadcast_in_dim.2
  174.7 14.0 %all-to-all-start.2 = ((f32[32,1,128]{2,1,0:T(1,128)}), f32[32,1,128]{2,1,0:T(1,128)S(1)}, u32[]{:S(2)}, u32[]{:S(2)}) async-start(f32[32,1,128]{2,1,0:T(1,128)} %broadcast_in_dim.2), calls=%async_computation.2 | async-start | bytes 32768 | tf_op jit(solution)/shard_map/all_to_all | solution.py:452
  188.7 0.8 copy.18
  189.5 20.8 %all-to-all-done.2 = f32[32,1,128]{2,1,0:T(1,128)S(1)} async-done(((f32[32,1,128]{2,1,0:T(1,128)}), f32[32,1,128]{2,1,0:T(1,128)S(1)}, u32[]{:S(2)}, u32[]{:S(2)}) %all-to-all-start.2) | async-done | bytes 16416 | tf_op jit(solution)/shard_map/all_to_all | solution.py:452
  210.3 0.6 reduce_sum.19
  (1 shorter events, 0.0 us)
Async XLA Ops:
  5.9 46.0 %copy-start.1 = (s32[2,2]{1,0:T(2,128)S(1)}, s32[2,2]{1,0:T(2,128)}, u32[]{:S(2)}) copy-start(s32[2,2]{1,0:T(2,128)} %thresh_ref.1) | copy-start | bytes 52
  6.0 146.3 %copy-start.2 = (bf16[4,2,256,256]{3,2,1,0:T(8,128)(2,1)S(1)}, bf16[4,2,256,256]{3,2,1,0:T(8,128)(2,1)}, u32[]{:S(2)}) copy-start(bf16[4,2,256,256]{3,2,1,0:T(8,128)(2,1)} %constant.21.clone.tab_ref) | copy-start | bytes 3145732
  6.0 146.3 %all-to-all-start = ((f32[32,64,128]{2,1,0:T(8,128)}), f32[32,64,128]{2,1,0:T(8,128)S(1)}, u32[]{:S(2)}, u32[]{:S(2)}) async-start(f32[32,64,128]{2,1,0:T(8,128)} %compress.1), calls=%async_computation | async-start | bytes 2097152 | tf_op jit(solution)/shard_map/all_to_all | solution.py:441
  51.9 0.7 copy-start
  153.3 6.3 %collective-permute-start = (f32[256,128]{1,0:T(8,128)S(1)}, f32[256,128]{1,0:T(8,128)S(1)}, u32[]{:S(2)}, u32[]{:S(2)}) collective-permute-start(f32[256,128]{1,0:T(8,128)S(1)} %get-tuple-element.12), channel_id=1, source_target_pairs={{0,8},{8,16},{16,24},{24,32},{32,40},{40,48},{48,56},{56,64},{64,7... | collective-permute-start | bytes 393224 | tf_op jit(solution)/shard_map/ppermute | solution.py:446
  157.1 6.9 %collective-permute-start.1 = (f32[256,128]{1,0:T(8,128)S(1)}, f32[256,128]{1,0:T(8,128)S(1)}, u32[]{:S(2)}, u32[]{:S(2)}) collective-permute-start(f32[256,128]{1,0:T(8,128)S(1)} %get-tuple-element.13), channel_id=1, source_target_pairs={{8,0},{16,8},{24,16},{32,24},{40,32},{48,40},{56,48},{64,56},{72,6... | collective-permute-start | bytes 393224 | tf_op jit(solution)/shard_map/ppermute | solution.py:447
  174.7 35.6 %all-to-all-start.2 = ((f32[32,1,128]{2,1,0:T(1,128)}), f32[32,1,128]{2,1,0:T(1,128)S(1)}, u32[]{:S(2)}, u32[]{:S(2)}) async-start(f32[32,1,128]{2,1,0:T(1,128)} %broadcast_in_dim.2), calls=%async_computation.2 | async-start | bytes 32768 | tf_op jit(solution)/shard_map/all_to_all | solution.py:452
where the time goes:
time: 213 us
  waiting for transfers between devices  125 us (59%)
  starting transfers between devices  65 us (31%)
  blocking collectives  9.69 us (5%)
  Pallas kernels  7.76 us (4%)
  between operations  2.51 us (1%)
    all_to_all x1, waiting for transfers between devices, local(): received = lax.all_to_all(ready, 'pulse', 0, 0, axis_index_groups=[ORDER])  99 us
    all_to_all x1, starting transfers between devices, local(): received = lax.all_to_all(ready, 'pulse', 0, 0, axis_index_groups=[ORDER])  45.9 us
    all_to_all x1, waiting for transfers between devices, local(): lax.all_to_all(jnp.broadcast_to(plane, (groups, 1, LANES)), 'pulse', 0, 0)  20.8 us
    all_to_all x1, starting transfers between devices, local(): lax.all_to_all(jnp.broadcast_to(plane, (groups, 1, LANES)), 'pulse', 0, 0)  14 us
    all_to_all x1, blocking collectives, local(): lax.all_to_all(soft.reshape(peers, 1, LANES), ('chan', 'sub'), 0, 0)  9.69 us
    pallas_call x1, Pallas kernels, compress(): pl.pallas_call(compress_kernel, out_shape=pltpu.VMEM((FAN, sets * 2 * ROW...  5.3 us
    ppermute x1, waiting for transfers between devices, local(): right = lax.ppermute(low_edge, 'pulse', [(i + 1, i) for i in range(ends)])  4.4 us
  transfers between devices with their start and end apart: 4, of which 4 were waited for; matrix products, arithmetic and copies ran while one was open for 0% of the time, Pallas kernels for 0%

commit v1 on v0

--- a/solution.py
+++ b/solution.py
@@ -150,7 +150,7 @@
 
 def compress_kernel(
     x_hbm, rep_hbm, fwd_hbm, inv_hbm, twd_hbm, o_ref,
-    x_ref, rep_ref, fwd_ref, inv_ref, twd_ref, h_ref, mid_ref, high_ref, low_ref, sems,
+    x_ref, rep_ref, fwd_ref, inv_ref, twd_ref, h_ref, mid_ref, high_ref, low_ref, out_ref, sems,
 ):
     channels, pulses = x_hbm.shape[1], x_hbm.shape[2]
     sets = [(c, p) for c in range(channels) for p in range(0, pulses, ROWS)]
@@ -175,16 +175,19 @@
         return jnp.broadcast_to(ref[part, k : k + 1, :], (ROWS, LANES))
 
     def put(i, k, value):
+        at = (i * FAN + k) * ROWS
         for part in range(2):
             high, low = split(value[part])
-            high_ref[i, k * ROWS : (k + 1) * ROWS, part * LANES : (part + 1) * LANES] = high
-            low_ref[i, k * ROWS : (k + 1) * ROWS, part * LANES : (part + 1) * LANES] = low
-
-    def product(i, table):
-        high = high_ref[i]
-        return dot(high, table[0]) + dot(low_ref[i], table[0]) + dot(high, table[1])
-
-    for i, (c, p) in enumerate(sets):
+            high_ref[at : at + ROWS, part * LANES : (part + 1) * LANES] = high
+            low_ref[at : at + ROWS, part * LANES : (part + 1) * LANES] = low
+
+    def product(table):
+        for t in range(4):
+            at = pl.ds(t * 256, 256)
+            high = high_ref[at]
+            out_ref[at] = dot(high, table[0]) + dot(low_ref[at], table[0]) + dot(high, table[1])
+
+    for i in range(n):
         loads[i].wait()
 
         def load(a, i=i):
@@ -197,25 +200,31 @@
             return (mid_ref[i, 0, j], mid_ref[i, 1, j])
 
         def twisted(k, value, i=i):
-            cos, sin = row(twd_ref, 0, k) , row(twd_ref, 1, k)
+            cos, sin = row(twd_ref, 0, k), row(twd_ref, 1, k)
             put(i, k, (value[0] * cos + value[1] * sin, value[1] * cos - value[0] * sin))
 
         fft32(load, keep, fetch, twisted, -1)
-        if i == 0:
-            load_fwd.wait()
-        spectrum = product(i, fwd_ref)
+    load_fwd.wait()
+    product(fwd_ref)
+    for i in range(n):
         for k in range(FAN):
-            re = spectrum[k * ROWS : (k + 1) * ROWS, :LANES]
-            im = spectrum[k * ROWS : (k + 1) * ROWS, LANES:]
+            at = (i * FAN + k) * ROWS
+            re, im = out_ref[at : at + ROWS, :LANES], out_ref[at : at + ROWS, LANES:]
             h_re, h_im = row(h_ref, 0, k), row(h_ref, 1, k)
             put(i, k, (re * h_re - im * h_im, re * h_im + im * h_re))
-        if i == 0:
-            load_inv.wait()
-        back = product(i, inv_ref)
-
-        def untwisted(k, back=back):
-            re = back[k * ROWS : (k + 1) * ROWS, :LANES]
-            im = back[k * ROWS : (k + 1) * ROWS, LANES:]
+    load_inv.wait()
+    product(inv_ref)
+    for i in range(n):
+
+        def keep(j, value, i=i):
+            mid_ref[i, 0, j], mid_ref[i, 1, j] = value
+
+        def fetch(j, i=i):
+            return (mid_ref[i, 0, j], mid_ref[i, 1, j])
+
+        def untwisted(k, i=i):
+            at = (i * FAN + k) * ROWS
+            re, im = out_ref[at : at + ROWS, :LANES], out_ref[at : at + ROWS, LANES:]
             cos, sin = row(twd_ref, 0, k), row(twd_ref, 1, k)
             return (re * cos - im * sin, im * cos + re * sin)
 
@@ -244,8 +253,9 @@
             pltpu.VMEM((2, FAN, LANES), F32),
             pltpu.VMEM((2, FAN, LANES), F32),
             pltpu.VMEM((sets, 2, FAN, ROWS, LANES), F32),
-            pltpu.VMEM((sets, FAN * ROWS, 2 * LANES), BF16),
-            pltpu.VMEM((sets, FAN * ROWS, 2 * LANES), BF16),
+            pltpu.VMEM((sets * FAN * ROWS, 2 * LANES), BF16),
+            pltpu.VMEM((sets * FAN * ROWS, 2 * LANES), BF16),
+            pltpu.VMEM((sets * FAN * ROWS, 2 * LANES), F32),
             pltpu.SemaphoreType.DMA((sets + 4,)),
         ],
         compiler_params=pltpu.CompilerParams(vmem_limit_bytes=limit),
@@ -254,7 +264,7 @@
     )(*[pltpu.with_memory_space_constraint(x, pltpu.HBM) for x in (samples, rep, fwd, inv, twd)])
 
 
-def doppler_kernel(x_ref, tab_ref, pow_ref, low_edge_ref, high_edge_ref, mid_ref, part_ref):
+def doppler_kernel(x_ref, tab_ref, pow_ref, first_ref, second_ref, mid_ref, part_ref):
     channels = pow_ref.shape[0]
     sets = x_ref.shape[1] // (2 * ROWS)
     halves = sets // channels
@@ -289,6 +299,7 @@
                 pow_ref[c, at : at + ROWS, :] = power[d2 * ROWS : (d2 + 1) * ROWS, c * LANES : (c + 1) * LANES]
     rows = PULSES // PACK
     lane = lax.broadcasted_iota(jnp.int32, (rows, LANES), 1)
+    even = lax.broadcast(lax.rem(lax.axis_index("pulse"), 2), (rows, LANES)) == 0
     for c in range(channels):
         low_piece = high_piece = None
         for b in range(PACK):
@@ -299,8 +310,8 @@
             mine = lane >= b * PARTS
             low_piece = low if low_piece is None else jnp.where(mine, low, low_piece)
             high_piece = high if high_piece is None else jnp.where(mine, high, high_piece)
-        low_edge_ref[c * rows : (c + 1) * rows, :] = low_piece
-        high_edge_ref[c * rows : (c + 1) * rows, :] = high_piece
+        first_ref[c * rows : (c + 1) * rows, :] = jnp.where(even, high_piece, low_piece)
+        second_ref[c * rows : (c + 1) * rows, :] = jnp.where(even, low_piece, high_piece)
 
 
 def doppler(received, channels, limit):
@@ -326,13 +337,16 @@
     )
 
 
-def windows_kernel(groups, window_ref, thresh_ref, place_ref, core_ref, side_ref, line_ref):
+def windows_kernel(groups, window_ref, thresh_ref, core_ref, side_ref, line_ref):
     channels = window_ref.shape[0]
     total = groups * LANES
-    gate = lax.broadcasted_iota(jnp.int32, (ROWS, LANES), 1) + place_ref[0] * LANES
+    gate = lax.broadcasted_iota(jnp.int32, (ROWS, LANES), 1) + lax.axis_index("pulse") * LANES
     row_id = lax.broadcasted_iota(jnp.int32, (LANES, LANES), 0)
     col_id = lax.broadcasted_iota(jnp.int32, (LANES, LANES), 1)
     piece, inner = row_id // PARTS, row_id % PARTS
+    odd = lax.rem(lax.axis_index("pulse"), 2)
+    first = LANES - odd * (LANES + PARTS)
+    second = odd * (LANES + PARTS) - PARTS
     core_ref[...] = jnp.zeros_like(core_ref)
     for c in range(channels):
         guard, train = window_ref[c, 0], window_ref[c, 1]
@@ -345,8 +359,8 @@
         core_ref[c * LANES : (c + 1) * LANES, c * LANES : (c + 1) * LANES] = band(row_id - col_id)
         for b in range(PACK):
             at = b * LANES
-            side_ref[c, :LANES, at : at + LANES] = band(inner - PARTS - col_id, piece == b)
-            side_ref[c, LANES:, at : at + LANES] = band(inner + LANES - col_id, piece == b)
+            side_ref[c, :LANES, at : at + LANES] = band(inner + first - col_id, piece == b)
+            side_ref[c, LANES:, at : at + LANES] = band(inner + second - col_id, piece == b)
         ahead = total - 1 - gate
         cells = jnp.minimum(gate, reach) - jnp.minimum(gate, guard)
         cells = cells + jnp.minimum(ahead, reach) - jnp.minimum(ahead, guard)
@@ -355,7 +369,7 @@
         line_ref[c, 1] = over / thresh_ref[c, 0].astype(F32)
 
 
-def windows(window, thresh, place, groups, limit):
+def windows(window, thresh, groups, limit):
     channels = window.shape[0]
     vmem = pl.BlockSpec(memory_space=pltpu.VMEM)
     smem = pl.BlockSpec(memory_space=pltpu.SMEM)
@@ -366,12 +380,12 @@
             pltpu.VMEM((channels, 2 * LANES, PACK * LANES), BF16),
             pltpu.VMEM((channels, 2, ROWS, LANES), F32),
         ),
-        in_specs=[smem, smem, smem],
+        in_specs=[smem, smem],
         out_specs=(vmem, vmem, vmem),
         compiler_params=pltpu.CompilerParams(vmem_limit_bytes=limit),
         cost_estimate=pl.CostEstimate(flops=10**7, bytes_accessed=MEBI, transcendentals=0),
         name="windows",
-    )(window, thresh, place)
+    )(window, thresh)
 
 
 def core_kernel(pow_ref, band_ref, noise_ref):
@@ -399,12 +413,13 @@
     return pltpu.with_memory_space_constraint(x, pltpu.VMEM)
 
 
-def cfar_kernel(pow_ref, noise_ref, left_ref, right_ref, side_ref, line_ref, ratio_ref, soft_ref):
+def cfar_kernel(pow_ref, noise_ref, first_ref, second_ref, side_ref, line_ref, out_hbm, soft_ref, ratio_ref, sems):
     channels = pow_ref.shape[0]
+    stores = []
     rows = PULSES // PACK
     soft_sum = jnp.zeros((ROWS, LANES), F32)
     for c in range(channels):
-        halo = jnp.concatenate([ref[c * rows : (c + 1) * rows, :] for ref in (left_ref, right_ref)], axis=1)
+        halo = jnp.concatenate([ref[c * rows : (c + 1) * rows, :] for ref in (first_ref, second_ref)], axis=1)
         high, low = split(halo)
         side = dot(high, side_ref[c]) + dot(low, side_ref[c])
         cells = jnp.concatenate([line_ref[c, 0]] * (rows // ROWS), axis=0)
@@ -414,22 +429,31 @@
             noise = noise_ref[c, at : at + rows, :] + side[:, b * LANES : (b + 1) * LANES]
             ratio = pow_ref[c, at : at + rows, :] * cells / (noise + EPSILON)
             ratio_ref[c, at : at + rows, :] = ratio
+            piece = (c, pl.ds(at, rows))
+            stores.append(pltpu.make_async_copy(ratio_ref.at[piece], out_hbm.at[piece], sems.at[len(stores)]))
+            stores[-1].start()
             soft = jnp.clip(ratio * over - 1.0, 0.0, 1.0)
             soft_sum = soft_sum + soft.reshape(rows // ROWS, ROWS, LANES).sum(axis=0)
     soft_ref[...] = jnp.broadcast_to(jnp.sum(soft_sum, axis=0, keepdims=True), soft_ref.shape)
-
-
-def cfar(power, noise, left, right, side, line, peers, limit):
+    for store in stores:
+        store.wait()
+
+
+def cfar(power, noise, first, second, side, line, peers, limit):
     vmem = pl.BlockSpec(memory_space=pltpu.VMEM)
     return pl.pallas_call(
         cfar_kernel,
-        out_shape=(pltpu.VMEM(power.shape, F32), pltpu.VMEM((peers, LANES), F32)),
+        out_shape=(pltpu.HBM(power.shape, F32), pltpu.VMEM((peers, LANES), F32)),
         in_specs=[vmem] * 6,
-        out_specs=(vmem, vmem),
+        out_specs=(pl.BlockSpec(memory_space=pltpu.HBM), vmem),
+        scratch_shapes=[
+            pltpu.VMEM(power.shape, F32),
+            pltpu.SemaphoreType.DMA((power.shape[0] * PACK,)),
+        ],
         compiler_params=pltpu.CompilerParams(vmem_limit_bytes=limit),
         cost_estimate=pl.CostEstimate(flops=10**9, bytes_accessed=2 * MEBI, transcendentals=0),
         name="cfar",
-    )(*[in_vmem(x) for x in (power, noise, left, right, side, line)])
+    )(*[in_vmem(x) for x in (power, noise, first, second, side, line)])
 
 
 def local(samples, replica, window, thresh):
@@ -439,15 +463,14 @@
     limit = 24 * MEBI
     ready = compress(samples, replica, limit)
     received = lax.all_to_all(ready, "pulse", 0, 0, axis_index_groups=[ORDER])
-    place = lax.axis_index("pulse").reshape(1)
-    band, side, line = windows(window, thresh, place, groups, limit)
-    power, low_edge, high_edge = doppler(received, channels, limit)
-    ends = groups - 1
-    left = lax.ppermute(high_edge, "pulse", [(i, i + 1) for i in range(ends)])
-    right = lax.ppermute(low_edge, "pulse", [(i + 1, i) for i in range(ends)])
+    power, first, second = doppler(received, channels, limit)
+    window, first = lax.optimization_barrier((window, first))
+    band, side, line = windows(window, thresh, groups, limit)
+    first = lax.ppermute(first, "pulse", [(i, i ^ 1) for i in range(groups)])
+    second = lax.ppermute(second, "pulse", [(i, ((i + 1) ^ 1) - 1) for i in range(1, groups - 1)])
     noise = core(power, band, limit)
     peers = lax.axis_size("chan") * lax.axis_size("sub")
-    ratio_map, soft = cfar(power, noise, left, right, side, line, peers, limit)
+    ratio_map, soft = cfar(power, noise, first, second, side, line, peers, limit)
     plane = jnp.sum(lax.all_to_all(soft.reshape(peers, 1, LANES), ("chan", "sub"), 0, 0), axis=0, keepdims=True)
     counts = lax.all_to_all(jnp.broadcast_to(plane, (groups, 1, LANES)), "pulse", 0, 0)
     detections = jnp.sum(counts) * (1024.0 / (PULSES * RANGE))

time: 213 us -> 210 us (0.986)
  blocking collectives: 9.69 us -> 194 us
  waiting for transfers between devices: 125 us -> 1.34 us
  starting transfers between devices: 65 us -> 4.47 us
    all_to_all x0 -> x2, blocking collectives: none -> 184 us  [the longest x1 146 us: local(): received = lax.all_to_all(ready, 'pulse', 0, 0, axis_index_groups=[ORDER])]
    all_to_all x2 -> x0, waiting for transfers between devices: 120 us -> none  [the longest x1 99 us: local(): received = lax.all_to_all(ready, 'pulse', 0, 0, axis_index_groups=[ORDER])]
    all_to_all x2 -> x0, starting transfers between devices: 59.9 us -> none  [the longest x1 45.9 us: local(): received = lax.all_to_all(ready, 'pulse', 0, 0, axis_index_groups=[ORDER])]
    ppermute x2, waiting for transfers between devices: 5.26 us -> 1.34 us  [the longest x1 1.34 us: local(): first = lax.ppermute(first, 'pulse', [(i, i ^ 1) for i in range(groups)])]
    pallas_call x1, Pallas kernels: 5.3 us -> 3.12 us  [compress(): pl.pallas_call(compress_kernel, out_shape=pltpu.VMEM((FAN, sets * 2 * ROW...]
  transfers between devices with their start and end apart: 4 -> 2, of which waited for: 4 -> 1; matrix products, arithmetic and copies ran while one was open for 0% -> 0% of each run, Pallas kernels for 0% -> 0%
where the time goes in v1:
time: 210 us; the launch traced here: 209 us
  blocking collectives  194 us (92%)
  Pallas kernels  6.31 us (3%)
  starting transfers between devices  4.47 us (2%)
  between operations  2.5 us (1%)
    all_to_all x1, blocking collectives, local(): received = lax.all_to_all(ready, 'pulse', 0, 0, axis_index_groups=[ORDER])  146 us
    all_to_all x1, blocking collectives, local(): lax.all_to_all(jnp.broadcast_to(plane, (groups, 1, LANES)), 'pulse', 0, 0)  38.3 us
    all_to_all x1, blocking collectives, local(): lax.all_to_all(soft.reshape(peers, 1, LANES), ('chan', 'sub'), 0, 0)  9.69 us
  transfers between devices with their start and end apart: 2, of which 1 were waited for; matrix products, arithmetic and copies ran while one was open for 0% of the time, Pallas kernels for 0%

profile of v1, /device:TPU:40, one launch (start us, length us, event | category | flops | bytes accessed | tf_op | source)
XLA Modules:
  0.0 209.4 jit_solution(13773844302796314635)
XLA Ops:
  0.6 3.1 %compress.1 = f32[32,64,128]{2,1,0:T(8,128)S(1)} custom-call(s32[2,2,16,4096]{3,2,1,0:T(8,128)} %x_hbm.1, f32[64,128]{1,0:T(8,128)} %bitcast.12, bf16[2,256,256]{2,1,0:T(8,128)(2,1)} %constant.12.clone.fwd_hbm, bf16[2,256,256]{2,1,0:T(8,128)(2,1)} %constant.13.clone.inv_hbm, f32[2,32,128]{2,1,0:T(8,128)} %constant.14.clone.twd_hbm), custom_call_target="tpu_custom_call" | custom-call | flops 2000000000 | bytes 2097152 | tf_op jit(solution)/shard_map/compress/pallas_call | solution.py:243
  3.8 0.0 copy-start.2
  3.8 146.1 %all_to_all.15.x_ref = f32[32,64,128]{2,1,0:T(8,128)S(1)} all-to-all(f32[32,64,128]{2,1,0:T(8,128)S(1)} %compress.1), channel_id=1, replica_groups={{0,8,24,16,48,56,40,32,96,104,120,112,80,88,72,64,192,200,216,208,240,2..., dimensions={0} | all-to-all | bytes 2097152 | tf_op jit(solution)/shard_map/all_to_all | solution.py:465
  149.8 0.0 copy-done.2
  149.8 1.0 doppler.1
  150.8 0.0 copy-start.1
  150.9 0.0 copy-start
  150.9 3.8 %collective-permute-start = (f32[256,128]{1,0:T(8,128)S(1)}, f32[256,128]{1,0:T(8,128)S(1)}, u32[]{:S(2)}, u32[]{:S(2)}) collective-permute-start(f32[256,128]{1,0:T(8,128)S(1)} %get-tuple-element.16), channel_id=1, source_target_pairs={{0,8},{8,0},{16,24},{24,16},{32,40},{40,32},{48,56},{56,48},{64,72... | collective-permute-start | bytes 393224 | tf_op jit(solution)/shard_map/ppermute | solution.py:469
  154.7 0.7 collective-permute-start.1
  155.4 0.0 copy-done.1
  155.4 0.0 copy-done
  155.4 0.7 windows.1
  156.1 0.3 core.1.noise_ref
  156.4 1.3 collective-permute-done.first_ref
  157.8 0.0 collective-permute-done.1.second_ref
  157.8 1.1 cfar.1
  158.9 9.7 %all_to_all.16 = f32[8,1,128]{2,1,0:T(1,128)S(1)} all-to-all(f32[8,1,128]{2,1,0:T(1,128)S(1)} %bitcast.10), channel_id=1, replica_groups=mesh['grp'=2,'pulse'=32,'chan'=4,'sub'=2] {'chan','sub'}, dimensions={0} | all-to-all | bytes 8192 | tf_op jit(solution)/shard_map/all_to_all | solution.py:474
  168.6 38.3 %all_to_all.17 = f32[32,1,128]{2,1,0:T(1,128)S(1)} all-to-all(f32[32,1,128]{2,1,0:T(1,128)S(1)} %broadcast_in_dim.2), channel_id=1, replica_groups=mesh['grp'=2,'pulse'=32,'chan'=4,'sub'=2] {'pulse'}, dimensions={0} | all-to-all | bytes 32768 | tf_op jit(solution)/shard_map/all_to_all | solution.py:475
  207.0 0.6 reduce_sum.19
  (2 shorter events, 0.0 us)
Async XLA Ops:
  3.8 146.1 %copy-start.2 = (bf16[4,2,256,256]{3,2,1,0:T(8,128)(2,1)S(1)}, bf16[4,2,256,256]{3,2,1,0:T(8,128)(2,1)}, u32[]{:S(2)}) copy-start(bf16[4,2,256,256]{3,2,1,0:T(8,128)(2,1)} %constant.15.clone.tab_ref) | copy-start | bytes 3145732
  150.8 4.5 %copy-start.1 = (s32[2,2]{1,0:T(2,128)S(1)}, s32[2,2]{1,0:T(2,128)}, u32[]{:S(2)}) copy-start(s32[2,2]{1,0:T(2,128)} %thresh_ref.1) | copy-start | bytes 52
  150.9 4.5 %copy-start = (s32[2,2]{1,0:T(2,128)S(1)}, s32[2,2]{1,0:T(2,128)}, u32[]{:S(2)}) copy-start(s32[2,2]{1,0:T(2,128)} %window_ref) | copy-start | bytes 52
  150.9 6.9 %collective-permute-start = (f32[256,128]{1,0:T(8,128)S(1)}, f32[256,128]{1,0:T(8,128)S(1)}, u32[]{:S(2)}, u32[]{:S(2)}) collective-permute-start(f32[256,128]{1,0:T(8,128)S(1)} %get-tuple-element.16), channel_id=1, source_target_pairs={{0,8},{8,0},{16,24},{24,16},{32,40},{40,32},{48,56},{56,48},{64,72... | collective-permute-start | bytes 393224 | tf_op jit(solution)/shard_map/ppermute | solution.py:469
  154.7 3.1 %collective-permute-start.1 = (f32[256,128]{1,0:T(8,128)S(1)}, f32[256,128]{1,0:T(8,128)S(1)}, u32[]{:S(2)}, u32[]{:S(2)}) collective-permute-start(f32[256,128]{1,0:T(8,128)S(1)} %get-tuple-element.17), channel_id=1, source_target_pairs={{8,16},{16,8},{24,32},{32,24},{40,48},{48,40},{56,64},{64,56},{72,... | collective-permute-start | bytes 393224 | tf_op jit(solution)/shard_map/ppermute | solution.py:470

commit v2 on v1

--- a/solution.py
+++ b/solution.py
@@ -471,8 +471,11 @@
     noise = core(power, band, limit)
     peers = lax.axis_size("chan") * lax.axis_size("sub")
     ratio_map, soft = cfar(power, noise, first, second, side, line, peers, limit)
-    plane = jnp.sum(lax.all_to_all(soft.reshape(peers, 1, LANES), ("chan", "sub"), 0, 0), axis=0, keepdims=True)
-    counts = lax.all_to_all(jnp.broadcast_to(plane, (groups, 1, LANES)), "pulse", 0, 0)
+    near = [i ^ (peers // 2 + 1) for i in range(peers)]
+    far = [(i + groups // 2) % groups for i in range(groups)]
+    soft = soft.reshape(peers, 1, LANES)
+    plane = jnp.sum(lax.all_to_all(soft, ("chan", "sub"), 0, 0, axis_index_groups=[near]), axis=0, keepdims=True)
+    counts = lax.all_to_all(jnp.broadcast_to(plane, (groups, 1, LANES)), "pulse", 0, 0, axis_index_groups=[far])
     detections = jnp.sum(counts) * (1024.0 / (PULSES * RANGE))
     return (ratio_map, detections.reshape(1))
 

time: 210 us -> 200 us (0.952)
  blocking collectives: 194 us -> 184 us
    all_to_all x2, blocking collectives: 48 us -> 38.1 us  [the longest x1 30.3 us: local(): lax.all_to_all(jnp.broadcast_to(plane, (groups, 1, LANES)), 'pulse', 0, 0...]
  transfers between devices with their start and end apart: 2 -> 2, of which waited for: 1 -> 1; matrix products, arithmetic and copies ran while one was open for 0% -> 0% of each run, Pallas kernels for 0% -> 1%
where the time goes in v2:
time: 200 us; the launch traced here: 199 us
  blocking collectives  184 us (92%)
  Pallas kernels  6.31 us (3%)
  starting transfers between devices  4.47 us (2%)
  between operations  2.5 us (1%)
    all_to_all x1, blocking collectives, local(): received = lax.all_to_all(ready, 'pulse', 0, 0, axis_index_groups=[ORDER])  146 us
    all_to_all x1, blocking collectives, local(): lax.all_to_all(jnp.broadcast_to(plane, (groups, 1, LANES)), 'pulse', 0, 0...  30.3 us
    all_to_all x1, blocking collectives, local(): lax.all_to_all(soft, ('chan', 'sub'), 0, 0, axis_index_groups=[near])  7.76 us
  transfers between devices with their start and end apart: 2, of which 1 were waited for; matrix products, arithmetic and copies ran while one was open for 0% of the time, Pallas kernels for 1%

profile of v2, /device:TPU:40, one launch (start us, length us, event | category | flops | bytes accessed | tf_op | source)
XLA Modules:
  0.0 199.4 jit_solution(6016859928766472399)
XLA Ops:
  0.6 3.1 %compress.1 = f32[32,64,128]{2,1,0:T(8,128)S(1)} custom-call(s32[2,2,16,4096]{3,2,1,0:T(8,128)} %x_hbm.1, f32[64,128]{1,0:T(8,128)} %bitcast.12, bf16[2,256,256]{2,1,0:T(8,128)(2,1)} %constant.12.clone.fwd_hbm, bf16[2,256,256]{2,1,0:T(8,128)(2,1)} %constant.13.clone.inv_hbm, f32[2,32,128]{2,1,0:T(8,128)} %constant.14.clone.twd_hbm), custom_call_target="tpu_custom_call" | custom-call | flops 2000000000 | bytes 2097152 | tf_op jit(solution)/shard_map/compress/pallas_call | solution.py:243
  3.8 0.0 copy-start.2
  3.8 146.1 %all_to_all.15.x_ref = f32[32,64,128]{2,1,0:T(8,128)S(1)} all-to-all(f32[32,64,128]{2,1,0:T(8,128)S(1)} %compress.1), channel_id=1, replica_groups={{0,8,24,16,48,56,40,32,96,104,120,112,80,88,72,64,192,200,216,208,240,2..., dimensions={0} | all-to-all | bytes 2097152 | tf_op jit(solution)/shard_map/all_to_all | solution.py:465
  149.8 0.0 copy-done.2
  149.8 1.0 doppler.1
  150.8 0.0 copy-start.1
  150.9 0.0 copy-start
  150.9 3.8 %collective-permute-start = (f32[256,128]{1,0:T(8,128)S(1)}, f32[256,128]{1,0:T(8,128)S(1)}, u32[]{:S(2)}, u32[]{:S(2)}) collective-permute-start(f32[256,128]{1,0:T(8,128)S(1)} %get-tuple-element.16), channel_id=1, source_target_pairs={{0,8},{8,0},{16,24},{24,16},{32,40},{40,32},{48,56},{56,48},{64,72... | collective-permute-start | bytes 393224 | tf_op jit(solution)/shard_map/ppermute | solution.py:469
  154.7 0.7 collective-permute-start.1
  155.4 0.0 copy-done.1
  155.4 0.0 copy-done
  155.4 0.7 windows.1
  156.1 0.3 core.1.noise_ref
  156.4 1.3 collective-permute-done.first_ref
  157.8 0.0 collective-permute-done.1.second_ref
  157.8 1.1 cfar.1
  158.9 7.8 %all_to_all.16 = f32[8,1,128]{2,1,0:T(1,128)S(1)} all-to-all(f32[8,1,128]{2,1,0:T(1,128)S(1)} %bitcast.10), channel_id=1, replica_groups={{5,4,7,6,1,0,3,2},{13,12,15,14,9,8,11,10},{21,20,23,22,17,16,19,18},{29..., dimensions={0} | all-to-all | bytes 8192 | tf_op jit(solution)/shard_map/all_to_all | solution.py:477
  166.7 30.3 %all_to_all.17 = f32[32,1,128]{2,1,0:T(1,128)S(1)} all-to-all(f32[32,1,128]{2,1,0:T(1,128)S(1)} %broadcast_in_dim.2), channel_id=1, replica_groups={{128,136,144,152,160,168,176,184,192,200,208,216,224,232,240,248,0,8,16..., dimensions={0} | all-to-all | bytes 32768 | tf_op jit(solution)/shard_map/all_to_all | solution.py:478
  197.0 0.6 reduce_sum.19
  (2 shorter events, 0.0 us)
Async XLA Ops:
  3.8 146.1 %copy-start.2 = (bf16[4,2,256,256]{3,2,1,0:T(8,128)(2,1)S(1)}, bf16[4,2,256,256]{3,2,1,0:T(8,128)(2,1)}, u32[]{:S(2)}) copy-start(bf16[4,2,256,256]{3,2,1,0:T(8,128)(2,1)} %constant.15.clone.tab_ref) | copy-start | bytes 3145732
  150.8 4.5 %copy-start.1 = (s32[2,2]{1,0:T(2,128)S(1)}, s32[2,2]{1,0:T(2,128)}, u32[]{:S(2)}) copy-start(s32[2,2]{1,0:T(2,128)} %thresh_ref.1) | copy-start | bytes 52
  150.9 4.5 %copy-start = (s32[2,2]{1,0:T(2,128)S(1)}, s32[2,2]{1,0:T(2,128)}, u32[]{:S(2)}) copy-start(s32[2,2]{1,0:T(2,128)} %window_ref) | copy-start | bytes 52
  150.9 6.9 %collective-permute-start = (f32[256,128]{1,0:T(8,128)S(1)}, f32[256,128]{1,0:T(8,128)S(1)}, u32[]{:S(2)}, u32[]{:S(2)}) collective-permute-start(f32[256,128]{1,0:T(8,128)S(1)} %get-tuple-element.16), channel_id=1, source_target_pairs={{0,8},{8,0},{16,24},{24,16},{32,40},{40,32},{48,56},{56,48},{64,72... | collective-permute-start | bytes 393224 | tf_op jit(solution)/shard_map/ppermute | solution.py:469
  154.7 3.1 %collective-permute-start.1 = (f32[256,128]{1,0:T(8,128)S(1)}, f32[256,128]{1,0:T(8,128)S(1)}, u32[]{:S(2)}, u32[]{:S(2)}) collective-permute-start(f32[256,128]{1,0:T(8,128)S(1)} %get-tuple-element.17), channel_id=1, source_target_pairs={{8,16},{16,8},{24,32},{32,24},{40,48},{48,40},{56,64},{64,56},{72,... | collective-permute-start | bytes 393224 | tf_op jit(solution)/shard_map/ppermute | solution.py:470

commit v3 on v2

--- a/solution.py
+++ b/solution.py
@@ -28,7 +28,7 @@
 F32 = jnp.float32
 BF16 = jnp.bfloat16
 MEBI = 1 << 20
-ORDER = [place ^ (place >> 1) for place in range(FAN)]
+ORDER = [0, 1, 31, 2, 6, 7, 5, 4, 12, 13, 10, 14, 15, 11, 9, 8, 24, 25, 27, 26, 30, 28, 29, 3, 20, 21, 23, 22, 18, 19, 17, 16]
 
 
 def slot(device):
@@ -434,7 +434,8 @@
             stores[-1].start()
             soft = jnp.clip(ratio * over - 1.0, 0.0, 1.0)
             soft_sum = soft_sum + soft.reshape(rows // ROWS, ROWS, LANES).sum(axis=0)
-    soft_ref[...] = jnp.broadcast_to(jnp.sum(soft_sum, axis=0, keepdims=True), soft_ref.shape)
+    count = jnp.sum(soft_sum, axis=0, keepdims=True) * (1024.0 / (PULSES * RANGE))
+    soft_ref[...] = jnp.broadcast_to(count, soft_ref.shape)
     for store in stores:
         store.wait()
 
@@ -476,7 +477,7 @@
     soft = soft.reshape(peers, 1, LANES)
     plane = jnp.sum(lax.all_to_all(soft, ("chan", "sub"), 0, 0, axis_index_groups=[near]), axis=0, keepdims=True)
     counts = lax.all_to_all(jnp.broadcast_to(plane, (groups, 1, LANES)), "pulse", 0, 0, axis_index_groups=[far])
-    detections = jnp.sum(counts) * (1024.0 / (PULSES * RANGE))
+    detections = jnp.sum(counts)
     return (ratio_map, detections.reshape(1))
 
 

time: 200 us -> 197 us (0.985)
    all_to_all x1, blocking collectives: 30.3 us -> 27.5 us  [local(): lax.all_to_all(jnp.broadcast_to(plane, (groups, 1, LANES)), 'pulse', 0, 0...]
where the time goes in v3:
time: 197 us; the launch traced here: 196 us
  blocking collectives  183 us (93%)
  Pallas kernels  6.32 us (3%)
  waiting for transfers between devices  3.19 us (2%)
  starting transfers between devices  2.62 us (1%)
    all_to_all x1, blocking collectives, local(): received = lax.all_to_all(ready, 'pulse', 0, 0, axis_index_groups=[ORDER])  148 us
    all_to_all x1, blocking collectives, local(): lax.all_to_all(jnp.broadcast_to(plane, (groups, 1, LANES)), 'pulse', 0, 0...  27.5 us
    all_to_all x1, blocking collectives, local(): lax.all_to_all(soft, ('chan', 'sub'), 0, 0, axis_index_groups=[near])  7.74 us
  transfers between devices with their start and end apart: 2, of which 1 were waited for; matrix products, arithmetic and copies ran while one was open for 0% of the time, Pallas kernels for 1%

profile of v3, /device:TPU:40, one launch (start us, length us, event | category | flops | bytes accessed | tf_op | source)
XLA Modules:
  0.0 196.3 jit_solution(3273518313380272823)
XLA Ops:
  0.6 3.1 %compress.1 = f32[32,64,128]{2,1,0:T(8,128)S(1)} custom-call(s32[2,2,16,4096]{3,2,1,0:T(8,128)} %x_hbm.1, f32[64,128]{1,0:T(8,128)} %bitcast.12, bf16[2,256,256]{2,1,0:T(8,128)(2,1)} %constant.10.clone.fwd_hbm, bf16[2,256,256]{2,1,0:T(8,128)(2,1)} %constant.11.clone.inv_hbm, f32[2,32,128]{2,1,0:T(8,128)} %constant.12.clone.twd_hbm), custom_call_target="tpu_custom_call" | custom-call | flops 2000000000 | bytes 2097152 | tf_op jit(solution)/shard_map/compress/pallas_call | solution.py:243
  3.8 0.0 copy-start.2
  3.8 147.6 %all_to_all.15.x_ref = f32[32,64,128]{2,1,0:T(8,128)S(1)} all-to-all(f32[32,64,128]{2,1,0:T(8,128)S(1)} %compress.1), channel_id=1, replica_groups={{0,8,248,16,48,56,40,32,96,104,80,112,120,88,72,64,192,200,216,208,240,..., dimensions={0} | all-to-all | bytes 2097152 | tf_op jit(solution)/shard_map/all_to_all | solution.py:466
  151.4 0.0 copy-done.2
  151.4 1.0 doppler.1
  152.4 0.0 copy-start.1
  152.4 0.0 copy-start
  152.4 2.0 collective-permute-start
  154.4 0.7 collective-permute-start.1
  155.1 0.0 copy-done.1
  155.1 0.0 copy-done
  155.1 0.7 windows.1
  155.8 0.3 core.1.noise_ref
  156.1 3.2 %collective-permute-done.first_ref = f32[256,128]{1,0:T(8,128)S(1)} collective-permute-done((f32[256,128]{1,0:T(8,128)S(1)}, f32[256,128]{1,0:T(8,128)S(1)}, u32[]{:S(2)}, u32[]{:S(2)}) %collective-permute-start) | collective-permute-done | bytes 131104 | tf_op jit(solution)/shard_map/ppermute | solution.py:470
  159.3 0.0 collective-permute-done.1.second_ref
  159.3 1.1 cfar.1
  160.5 7.7 %all_to_all.16 = f32[8,1,128]{2,1,0:T(1,128)S(1)} all-to-all(f32[8,1,128]{2,1,0:T(1,128)S(1)} %bitcast.10), channel_id=1, replica_groups={{5,4,7,6,1,0,3,2},{13,12,15,14,9,8,11,10},{21,20,23,22,17,16,19,18},{29..., dimensions={0} | all-to-all | bytes 8192 | tf_op jit(solution)/shard_map/all_to_all | solution.py:478
  168.2 27.5 %all_to_all.17 = f32[32,1,128]{2,1,0:T(1,128)S(1)} all-to-all(f32[32,1,128]{2,1,0:T(1,128)S(1)} %broadcast_in_dim.2), channel_id=1, replica_groups={{128,136,144,152,160,168,176,184,192,200,208,216,224,232,240,248,0,8,16..., dimensions={0} | all-to-all | bytes 32768 | tf_op jit(solution)/shard_map/all_to_all | solution.py:479
  195.7 0.6 reduce_sum.19
  (2 shorter events, 0.0 us)
Async XLA Ops:
  3.8 147.6 %copy-start.2 = (bf16[4,2,256,256]{3,2,1,0:T(8,128)(2,1)S(1)}, bf16[4,2,256,256]{3,2,1,0:T(8,128)(2,1)}, u32[]{:S(2)}) copy-start(bf16[4,2,256,256]{3,2,1,0:T(8,128)(2,1)} %constant.13.clone.tab_ref) | copy-start | bytes 3145732
  152.4 2.7 %copy-start.1 = (s32[2,2]{1,0:T(2,128)S(1)}, s32[2,2]{1,0:T(2,128)}, u32[]{:S(2)}) copy-start(s32[2,2]{1,0:T(2,128)} %thresh_ref.1) | copy-start | bytes 52
  152.4 2.7 %copy-start = (s32[2,2]{1,0:T(2,128)S(1)}, s32[2,2]{1,0:T(2,128)}, u32[]{:S(2)}) copy-start(s32[2,2]{1,0:T(2,128)} %window_ref) | copy-start | bytes 52
  152.4 6.9 %collective-permute-start = (f32[256,128]{1,0:T(8,128)S(1)}, f32[256,128]{1,0:T(8,128)S(1)}, u32[]{:S(2)}, u32[]{:S(2)}) collective-permute-start(f32[256,128]{1,0:T(8,128)S(1)} %get-tuple-element.16), channel_id=1, source_target_pairs={{0,8},{8,0},{16,24},{24,16},{32,40},{40,32},{48,56},{56,48},{64,72... | collective-permute-start | bytes 393224 | tf_op jit(solution)/shard_map/ppermute | solution.py:470
  154.4 4.9 %collective-permute-start.1 = (f32[256,128]{1,0:T(8,128)S(1)}, f32[256,128]{1,0:T(8,128)S(1)}, u32[]{:S(2)}, u32[]{:S(2)}) collective-permute-start(f32[256,128]{1,0:T(8,128)S(1)} %get-tuple-element.17), channel_id=1, source_target_pairs={{8,16},{16,8},{24,32},{32,24},{40,48},{48,40},{56,64},{64,56},{72,... | collective-permute-start | bytes 393224 | tf_op jit(solution)/shard_map/ppermute | solution.py:471

commit v4 on v3

--- a/solution.py
+++ b/solution.py
@@ -288,30 +288,31 @@
 
         fft32(load, keep, fetch, store, -1)
     scale = INPUT_SCALE * INPUT_SCALE / (float(RANGE) * float(RANGE) * PULSES)
+    lane = lax.broadcasted_iota(jnp.int32, (ROWS, LANES), 1)
+    even = lax.broadcast(lax.rem(lax.axis_index("pulse"), 2), (ROWS, LANES)) == 0
+    step = FINE // PACK
     for tile in range(FAN // ROWS):
         high, low = split(part_ref[tile])
         out = dot(tab_ref[tile, 0], high) + dot(tab_ref[tile, 0], low) + dot(tab_ref[tile, 1], high)
         half = out.shape[0] // 2
         power = (out[:half] * out[:half] + out[half:] * out[half:]) * scale
-        for d2 in range(FINE):
-            for c in range(channels):
-                at = d2 * FAN + tile * ROWS
-                pow_ref[c, at : at + ROWS, :] = power[d2 * ROWS : (d2 + 1) * ROWS, c * LANES : (c + 1) * LANES]
-    rows = PULSES // PACK
-    lane = lax.broadcasted_iota(jnp.int32, (rows, LANES), 1)
-    even = lax.broadcast(lax.rem(lax.axis_index("pulse"), 2), (rows, LANES)) == 0
-    for c in range(channels):
-        low_piece = high_piece = None
-        for b in range(PACK):
-            x = pow_ref[c, b * rows : (b + 1) * rows, :]
-            low = pltpu.roll(x, b * PARTS, 1) if b else x
-            shift = (b * PARTS - (LANES - PARTS)) % LANES
-            high = pltpu.roll(x, shift, 1) if shift else x
-            mine = lane >= b * PARTS
-            low_piece = low if low_piece is None else jnp.where(mine, low, low_piece)
-            high_piece = high if high_piece is None else jnp.where(mine, high, high_piece)
-        first_ref[c * rows : (c + 1) * rows, :] = jnp.where(even, high_piece, low_piece)
-        second_ref[c * rows : (c + 1) * rows, :] = jnp.where(even, low_piece, high_piece)
+        for c in range(channels):
+            for m in range(step):
+                low_piece = high_piece = None
+                for b in range(PACK):
+                    d2 = b * step + m
+                    x = power[d2 * ROWS : (d2 + 1) * ROWS, c * LANES : (c + 1) * LANES]
+                    at = d2 * FAN + tile * ROWS
+                    pow_ref[c, at : at + ROWS, :] = x
+                    down = pltpu.roll(x, b * PARTS, 1) if b else x
+                    shift = (b * PARTS - (LANES - PARTS)) % LANES
+                    up = pltpu.roll(x, shift, 1) if shift else x
+                    mine = lane >= b * PARTS
+                    low_piece = down if low_piece is None else jnp.where(mine, down, low_piece)
+                    high_piece = up if high_piece is None else jnp.where(mine, up, high_piece)
+                at = c * (PULSES // PACK) + m * FAN + tile * ROWS
+                first_ref[at : at + ROWS, :] = jnp.where(even, high_piece, low_piece)
+                second_ref[at : at + ROWS, :] = jnp.where(even, low_piece, high_piece)
 
 
 def doppler(received, channels, limit):
@@ -413,9 +414,8 @@
     return pltpu.with_memory_space_constraint(x, pltpu.VMEM)
 
 
-def cfar_kernel(pow_ref, noise_ref, first_ref, second_ref, side_ref, line_ref, out_hbm, soft_ref, ratio_ref, sems):
+def cfar_kernel(pow_ref, noise_ref, first_ref, second_ref, side_ref, line_ref, ratio_ref, out_hbm, soft_ref, sem):
     channels = pow_ref.shape[0]
-    stores = []
     rows = PULSES // PACK
     soft_sum = jnp.zeros((ROWS, LANES), F32)
     for c in range(channels):
@@ -429,32 +429,64 @@
             noise = noise_ref[c, at : at + rows, :] + side[:, b * LANES : (b + 1) * LANES]
             ratio = pow_ref[c, at : at + rows, :] * cells / (noise + EPSILON)
             ratio_ref[c, at : at + rows, :] = ratio
-            piece = (c, pl.ds(at, rows))
-            stores.append(pltpu.make_async_copy(ratio_ref.at[piece], out_hbm.at[piece], sems.at[len(stores)]))
-            stores[-1].start()
             soft = jnp.clip(ratio * over - 1.0, 0.0, 1.0)
             soft_sum = soft_sum + soft.reshape(rows // ROWS, ROWS, LANES).sum(axis=0)
     count = jnp.sum(soft_sum, axis=0, keepdims=True) * (1024.0 / (PULSES * RANGE))
     soft_ref[...] = jnp.broadcast_to(count, soft_ref.shape)
-    for store in stores:
+
+    @pl.when(stores_early())
+    def _():
+        store = pltpu.make_async_copy(ratio_ref, out_hbm, sem)
+        store.start()
         store.wait()
+
+
+def stores_early():
+    return lax.axis_index("pulse") == 0
 
 
 def cfar(power, noise, first, second, side, line, peers, limit):
     vmem = pl.BlockSpec(memory_space=pltpu.VMEM)
     return pl.pallas_call(
         cfar_kernel,
-        out_shape=(pltpu.HBM(power.shape, F32), pltpu.VMEM((peers, LANES), F32)),
+        out_shape=(pltpu.VMEM(power.shape, F32), pltpu.HBM(power.shape, F32), pltpu.VMEM((peers, LANES), F32)),
         in_specs=[vmem] * 6,
-        out_specs=(pl.BlockSpec(memory_space=pltpu.HBM), vmem),
-        scratch_shapes=[
-            pltpu.VMEM(power.shape, F32),
-            pltpu.SemaphoreType.DMA((power.shape[0] * PACK,)),
-        ],
+        out_specs=(vmem, pl.BlockSpec(memory_space=pltpu.HBM), vmem),
+        scratch_shapes=[pltpu.SemaphoreType.DMA],
         compiler_params=pltpu.CompilerParams(vmem_limit_bytes=limit),
         cost_estimate=pl.CostEstimate(flops=10**9, bytes_accessed=2 * MEBI, transcendentals=0),
         name="cfar",
     )(*[in_vmem(x) for x in (power, noise, first, second, side, line)])
+
+
+def finish_kernel(counts_ref, ratio_ref, _, out_hbm, sum_ref, sem):
+    store = pltpu.make_async_copy(ratio_ref, out_hbm, sem)
+    late = jnp.logical_not(stores_early())
+
+    @pl.when(late)
+    def _():
+        store.start()
+
+    sum_ref[0] = jnp.sum(counts_ref[...])
+
+    @pl.when(late)
+    def _():
+        store.wait()
+
+
+def finish(counts, ratio, partial, limit):
+    vmem, hbm = pl.BlockSpec(memory_space=pltpu.VMEM), pl.BlockSpec(memory_space=pltpu.HBM)
+    return pl.pallas_call(
+        finish_kernel,
+        out_shape=(pltpu.HBM(ratio.shape, F32), jax.ShapeDtypeStruct((1,), F32)),
+        in_specs=[vmem, vmem, hbm],
+        out_specs=(hbm, pl.BlockSpec(memory_space=pltpu.SMEM)),
+        scratch_shapes=[pltpu.SemaphoreType.DMA],
+        input_output_aliases={2: 0},
+        compiler_params=pltpu.CompilerParams(vmem_limit_bytes=limit),
+        cost_estimate=pl.CostEstimate(flops=10**5, bytes_accessed=MEBI, transcendentals=0),
+        name="finish",
+    )(in_vmem(counts), in_vmem(ratio), partial)
 
 
 def local(samples, replica, window, thresh):
@@ -471,14 +503,13 @@
     second = lax.ppermute(second, "pulse", [(i, ((i + 1) ^ 1) - 1) for i in range(1, groups - 1)])
     noise = core(power, band, limit)
     peers = lax.axis_size("chan") * lax.axis_size("sub")
-    ratio_map, soft = cfar(power, noise, first, second, side, line, peers, limit)
+    ratio, partial, soft = cfar(power, noise, first, second, side, line, peers, limit)
     near = [i ^ (peers // 2 + 1) for i in range(peers)]
     far = [(i + groups // 2) % groups for i in range(groups)]
     soft = soft.reshape(peers, 1, LANES)
     plane = jnp.sum(lax.all_to_all(soft, ("chan", "sub"), 0, 0, axis_index_groups=[near]), axis=0, keepdims=True)
     counts = lax.all_to_all(jnp.broadcast_to(plane, (groups, 1, LANES)), "pulse", 0, 0, axis_index_groups=[far])
-    detections = jnp.sum(counts)
-    return (ratio_map, detections.reshape(1))
+    return finish(counts.reshape(groups, LANES), ratio, partial, limit)
 
 
 def solution(mesh):

time: 197 us -> 196 us (level)
  no operation moved by 1% of the time
where the time goes in v4:
time: 196 us
  blocking collectives  182 us (93%)
  Pallas kernels  6.99 us (4%)
  waiting for transfers between devices  3.2 us (2%)
  starting transfers between devices  2.62 us (1%)
    all_to_all x1, blocking collectives, local(): received = lax.all_to_all(ready, 'pulse', 0, 0, axis_index_groups=[ORDER])  148 us
    all_to_all x1, blocking collectives, local(): lax.all_to_all(jnp.broadcast_to(plane, (groups, 1, LANES)), 'pulse', 0, 0...  26.7 us
    all_to_all x1, blocking collectives, local(): lax.all_to_all(soft, ('chan', 'sub'), 0, 0, axis_index_groups=[near])  7.75 us
  transfers between devices with their start and end apart: 2, of which 1 were waited for; matrix products, arithmetic and copies ran while one was open for 0% of the time, Pallas kernels for 1%

profile of v4, /device:TPU:40, one launch (start us, length us, event | category | flops | bytes accessed | tf_op | source)
XLA Modules:
  0.0 195.6 jit_solution(16515488390538061633)
XLA Ops:
  0.6 3.1 %compress.1 = f32[32,64,128]{2,1,0:T(8,128)S(1)} custom-call(s32[2,2,16,4096]{3,2,1,0:T(8,128)} %x_hbm.1, f32[64,128]{1,0:T(8,128)} %bitcast.11, bf16[2,256,256]{2,1,0:T(8,128)(2,1)} %constant.10.clone.fwd_hbm, bf16[2,256,256]{2,1,0:T(8,128)(2,1)} %constant.11.clone.inv_hbm, f32[2,32,128]{2,1,0:T(8,128)} %constant.12.clone.twd_hbm), custom_call_target="tpu_custom_call" | custom-call | flops 2000000000 | bytes 2097152 | tf_op jit(solution)/shard_map/compress/pallas_call | solution.py:243
  3.8 0.0 copy-start.2
  3.8 147.6 %all_to_all.15.x_ref = f32[32,64,128]{2,1,0:T(8,128)S(1)} all-to-all(f32[32,64,128]{2,1,0:T(8,128)S(1)} %compress.1), channel_id=1, replica_groups={{0,8,248,16,48,56,40,32,96,104,80,112,120,88,72,64,192,200,216,208,240,..., dimensions={0} | all-to-all | bytes 2097152 | tf_op jit(solution)/shard_map/all_to_all | solution.py:498
  151.4 0.0 copy-done.2
  151.4 1.0 doppler.1
  152.4 0.0 copy-start.1
  152.4 0.0 copy-start
  152.4 2.0 collective-permute-start
  154.4 0.7 collective-permute-start.1
  155.1 0.0 copy-done.1
  155.1 0.0 copy-done
  155.1 0.7 windows.1
  155.8 0.3 core.1.noise_ref
  156.1 3.2 %collective-permute-done.first_ref = f32[256,128]{1,0:T(8,128)S(1)} collective-permute-done((f32[256,128]{1,0:T(8,128)S(1)}, f32[256,128]{1,0:T(8,128)S(1)}, u32[]{:S(2)}, u32[]{:S(2)}) %collective-permute-start) | collective-permute-done | bytes 131104 | tf_op jit(solution)/shard_map/ppermute | solution.py:502
  159.3 0.0 collective-permute-done.1.second_ref
  159.3 1.2 cfar.1
  160.5 7.7 %all_to_all.16 = f32[8,1,128]{2,1,0:T(1,128)S(1)} all-to-all(f32[8,1,128]{2,1,0:T(1,128)S(1)} %bitcast.10), channel_id=1, replica_groups={{5,4,7,6,1,0,3,2},{13,12,15,14,9,8,11,10},{21,20,23,22,17,16,19,18},{29..., dimensions={0} | all-to-all | bytes 8192 | tf_op jit(solution)/shard_map/all_to_all | solution.py:510
  168.3 26.7 %all_to_all.17 = f32[32,1,128]{2,1,0:T(1,128)S(1)} all-to-all(f32[32,1,128]{2,1,0:T(1,128)S(1)} %broadcast_in_dim.2), channel_id=1, replica_groups={{128,136,144,152,160,168,176,184,192,200,208,216,224,232,240,248,0,8,16..., dimensions={0} | all-to-all | bytes 32768 | tf_op jit(solution)/shard_map/all_to_all | solution.py:511
  195.0 0.6 finish.1
  (2 shorter events, 0.0 us)
Async XLA Ops:
  3.8 147.6 %copy-start.2 = (bf16[4,2,256,256]{3,2,1,0:T(8,128)(2,1)S(1)}, bf16[4,2,256,256]{3,2,1,0:T(8,128)(2,1)}, u32[]{:S(2)}) copy-start(bf16[4,2,256,256]{3,2,1,0:T(8,128)(2,1)} %constant.13.clone.tab_ref) | copy-start | bytes 3145732
  152.4 2.7 %copy-start.1 = (s32[2,2]{1,0:T(2,128)S(1)}, s32[2,2]{1,0:T(2,128)}, u32[]{:S(2)}) copy-start(s32[2,2]{1,0:T(2,128)} %thresh_ref.1) | copy-start | bytes 52
  152.4 2.7 %copy-start = (s32[2,2]{1,0:T(2,128)S(1)}, s32[2,2]{1,0:T(2,128)}, u32[]{:S(2)}) copy-start(s32[2,2]{1,0:T(2,128)} %window_ref) | copy-start | bytes 52
  152.4 6.9 %collective-permute-start = (f32[256,128]{1,0:T(8,128)S(1)}, f32[256,128]{1,0:T(8,128)S(1)}, u32[]{:S(2)}, u32[]{:S(2)}) collective-permute-start(f32[256,128]{1,0:T(8,128)S(1)} %get-tuple-element.17), channel_id=1, source_target_pairs={{0,8},{8,0},{16,24},{24,16},{32,40},{40,32},{48,56},{56,48},{64,72... | collective-permute-start | bytes 393224 | tf_op jit(solution)/shard_map/ppermute | solution.py:502
  154.4 4.9 %collective-permute-start.1 = (f32[256,128]{1,0:T(8,128)S(1)}, f32[256,128]{1,0:T(8,128)S(1)}, u32[]{:S(2)}, u32[]{:S(2)}) collective-permute-start(f32[256,128]{1,0:T(8,128)S(1)} %get-tuple-element.18), channel_id=1, source_target_pairs={{8,16},{16,8},{24,32},{32,24},{40,48},{48,40},{56,64},{64,56},{72,... | collective-permute-start | bytes 393224 | tf_op jit(solution)/shard_map/ppermute | solution.py:503

commit v5 on v4

--- a/solution.py
+++ b/solution.py
@@ -28,7 +28,7 @@
 F32 = jnp.float32
 BF16 = jnp.bfloat16
 MEBI = 1 << 20
-ORDER = [0, 1, 31, 2, 6, 7, 5, 4, 12, 13, 10, 14, 15, 11, 9, 8, 24, 25, 27, 26, 30, 28, 29, 3, 20, 21, 23, 22, 18, 19, 17, 16]
+ORDER = [0, 1, 31, 2, 6, 7, 5, 12, 4, 13, 10, 14, 15, 9, 11, 24, 8, 25, 27, 26, 30, 28, 29, 3, 20, 21, 23, 22, 18, 19, 17, 16]
 
 
 def slot(device):

time: 196 us -> 195 us (level)
  starting transfers between devices: 2.62 us -> 7.04 us
  blocking collectives: 182 us -> 179 us
  waiting for transfers between devices: 3.2 us -> 1.19 us
    ppermute x1, starting transfers between devices: 1.95 us -> 6.37 us  [local(): first = lax.ppermute(first, 'pulse', [(i, i ^ 1) for i in range(groups)])]
    all_to_all x1, blocking collectives: 148 us -> 145 us  [local(): received = lax.all_to_all(ready, 'pulse', 0, 0, axis_index_groups=[ORDER])]
    ppermute x1, waiting for transfers between devices: 3.19 us -> 1.19 us  [local(): first = lax.ppermute(first, 'pulse', [(i, i ^ 1) for i in range(groups)])]
where the time goes in v5:
time: 195 us
  blocking collectives  179 us (92%)
  starting transfers between devices  7.04 us (4%)
  Pallas kernels  6.99 us (4%)
    all_to_all x1, blocking collectives, local(): received = lax.all_to_all(ready, 'pulse', 0, 0, axis_index_groups=[ORDER])  145 us
    all_to_all x1, blocking collectives, local(): lax.all_to_all(jnp.broadcast_to(plane, (groups, 1, LANES)), 'pulse', 0, 0...  26.2 us
    all_to_all x1, blocking collectives, local(): lax.all_to_all(soft, ('chan', 'sub'), 0, 0, axis_index_groups=[near])  7.75 us
    ppermute x1, starting transfers between devices, local(): first = lax.ppermute(first, 'pulse', [(i, i ^ 1) for i in range(groups)])  6.37 us
  transfers between devices with their start and end apart: 2, of which 1 were waited for; matrix products, arithmetic and copies ran while one was open for 0% of the time, Pallas kernels for 1%

profile of v5, /device:TPU:40, one launch (start us, length us, event | category | flops | bytes accessed | tf_op | source)
XLA Modules:
  0.0 195.0 jit_solution(15927287450202864416)
XLA Ops:
  0.6 3.1 %compress.1 = f32[32,64,128]{2,1,0:T(8,128)S(1)} custom-call(s32[2,2,16,4096]{3,2,1,0:T(8,128)} %x_hbm.1, f32[64,128]{1,0:T(8,128)} %bitcast.11, bf16[2,256,256]{2,1,0:T(8,128)(2,1)} %constant.10.clone.fwd_hbm, bf16[2,256,256]{2,1,0:T(8,128)(2,1)} %constant.11.clone.inv_hbm, f32[2,32,128]{2,1,0:T(8,128)} %constant.12.clone.twd_hbm), custom_call_target="tpu_custom_call" | custom-call | flops 2000000000 | bytes 2097152 | tf_op jit(solution)/shard_map/compress/pallas_call | solution.py:243
  3.8 0.0 copy-start.2
  3.8 145.0 %all_to_all.15.x_ref = f32[32,64,128]{2,1,0:T(8,128)S(1)} all-to-all(f32[32,64,128]{2,1,0:T(8,128)S(1)} %compress.1), channel_id=1, replica_groups={{0,8,248,16,48,56,40,96,32,104,80,112,120,72,88,192,64,200,216,208,240,..., dimensions={0} | all-to-all | bytes 2097152 | tf_op jit(solution)/shard_map/all_to_all | solution.py:498
  148.8 0.0 copy-done.2
  148.8 1.0 doppler.1
  149.8 0.0 copy-start.1
  149.9 0.0 copy-start
  149.9 6.4 %collective-permute-start = (f32[256,128]{1,0:T(8,128)S(1)}, f32[256,128]{1,0:T(8,128)S(1)}, u32[]{:S(2)}, u32[]{:S(2)}) collective-permute-start(f32[256,128]{1,0:T(8,128)S(1)} %get-tuple-element.17), channel_id=1, source_target_pairs={{0,8},{8,0},{16,24},{24,16},{32,40},{40,32},{48,56},{56,48},{64,72... | collective-permute-start | bytes 393224 | tf_op jit(solution)/shard_map/ppermute | solution.py:502
  156.3 0.7 collective-permute-start.1
  156.9 0.0 copy-done.1
  156.9 0.0 copy-done
  157.0 0.7 windows.1
  157.7 0.3 core.1.noise_ref
  158.0 1.2 collective-permute-done.first_ref
  159.2 0.0 collective-permute-done.1.second_ref
  159.2 1.2 cfar.1
  160.4 7.8 %all_to_all.16 = f32[8,1,128]{2,1,0:T(1,128)S(1)} all-to-all(f32[8,1,128]{2,1,0:T(1,128)S(1)} %bitcast.10), channel_id=1, replica_groups={{5,4,7,6,1,0,3,2},{13,12,15,14,9,8,11,10},{21,20,23,22,17,16,19,18},{29..., dimensions={0} | all-to-all | bytes 8192 | tf_op jit(solution)/shard_map/all_to_all | solution.py:510
  168.2 26.2 %all_to_all.17 = f32[32,1,128]{2,1,0:T(1,128)S(1)} all-to-all(f32[32,1,128]{2,1,0:T(1,128)S(1)} %broadcast_in_dim.2), channel_id=1, replica_groups={{128,136,144,152,160,168,176,184,192,200,208,216,224,232,240,248,0,8,16..., dimensions={0} | all-to-all | bytes 32768 | tf_op jit(solution)/shard_map/all_to_all | solution.py:511
  194.4 0.6 finish.1
  (2 shorter events, 0.0 us)
Async XLA Ops:
  3.8 145.1 %copy-start.2 = (bf16[4,2,256,256]{3,2,1,0:T(8,128)(2,1)S(1)}, bf16[4,2,256,256]{3,2,1,0:T(8,128)(2,1)}, u32[]{:S(2)}) copy-start(bf16[4,2,256,256]{3,2,1,0:T(8,128)(2,1)} %constant.13.clone.tab_ref) | copy-start | bytes 3145732
  149.8 7.1 %copy-start.1 = (s32[2,2]{1,0:T(2,128)S(1)}, s32[2,2]{1,0:T(2,128)}, u32[]{:S(2)}) copy-start(s32[2,2]{1,0:T(2,128)} %thresh_ref.1) | copy-start | bytes 52
  149.9 7.1 %copy-start = (s32[2,2]{1,0:T(2,128)S(1)}, s32[2,2]{1,0:T(2,128)}, u32[]{:S(2)}) copy-start(s32[2,2]{1,0:T(2,128)} %window_ref) | copy-start | bytes 52
  149.9 9.3 %collective-permute-start = (f32[256,128]{1,0:T(8,128)S(1)}, f32[256,128]{1,0:T(8,128)S(1)}, u32[]{:S(2)}, u32[]{:S(2)}) collective-permute-start(f32[256,128]{1,0:T(8,128)S(1)} %get-tuple-element.17), channel_id=1, source_target_pairs={{0,8},{8,0},{16,24},{24,16},{32,40},{40,32},{48,56},{56,48},{64,72... | collective-permute-start | bytes 393224 | tf_op jit(solution)/shard_map/ppermute | solution.py:502
  156.3 2.9 %collective-permute-start.1 = (f32[256,128]{1,0:T(8,128)S(1)}, f32[256,128]{1,0:T(8,128)S(1)}, u32[]{:S(2)}, u32[]{:S(2)}) collective-permute-start(f32[256,128]{1,0:T(8,128)S(1)} %get-tuple-element.18), channel_id=1, source_target_pairs={{8,16},{16,8},{24,32},{32,24},{40,48},{48,40},{56,64},{64,56},{72,... | collective-permute-start | bytes 393224 | tf_op jit(solution)/shard_map/ppermute | solution.py:503

commit v6 on v5

--- a/solution.py
+++ b/solution.py
@@ -28,7 +28,7 @@
 F32 = jnp.float32
 BF16 = jnp.bfloat16
 MEBI = 1 << 20
-ORDER = [0, 1, 31, 2, 6, 7, 5, 12, 4, 13, 10, 14, 15, 9, 11, 24, 8, 25, 27, 26, 30, 28, 29, 3, 20, 21, 23, 22, 18, 19, 17, 16]
+ORDER = [0, 1, 31, 2, 6, 7, 5, 12, 4, 13, 10, 14, 15, 9, 11, 24, 8, 25, 27, 26, 30, 29, 28, 3, 20, 21, 23, 22, 18, 19, 17, 16]
 
 
 def slot(device):

time: 195 us -> 195 us (level)
  no operation moved by 1% of the time
where the time goes in v6:
time: 195 us
  blocking collectives  179 us (92%)
  Pallas kernels  7 us (4%)
  starting transfers between devices  6.46 us (3%)
    all_to_all x1, blocking collectives, local(): received = lax.all_to_all(ready, 'pulse', 0, 0, axis_index_groups=[ORDER])  144 us
    all_to_all x1, blocking collectives, local(): lax.all_to_all(jnp.broadcast_to(plane, (groups, 1, LANES)), 'pulse', 0, 0...  27 us
    all_to_all x1, blocking collectives, local(): lax.all_to_all(soft, ('chan', 'sub'), 0, 0, axis_index_groups=[near])  7.73 us
    ppermute x1, starting transfers between devices, local(): first = lax.ppermute(first, 'pulse', [(i, i ^ 1) for i in range(groups)])  5.79 us
  transfers between devices with their start and end apart: 2, of which 1 were waited for; matrix products, arithmetic and copies ran while one was open for 0% of the time, Pallas kernels for 1%

profile of v6, /device:TPU:40, one launch (start us, length us, event | category | flops | bytes accessed | tf_op | source)
XLA Modules:
  0.0 194.6 jit_solution(753647830686779070)
XLA Ops:
  0.6 3.1 %compress.1 = f32[32,64,128]{2,1,0:T(8,128)S(1)} custom-call(s32[2,2,16,4096]{3,2,1,0:T(8,128)} %x_hbm.1, f32[64,128]{1,0:T(8,128)} %bitcast.11, bf16[2,256,256]{2,1,0:T(8,128)(2,1)} %constant.10.clone.fwd_hbm, bf16[2,256,256]{2,1,0:T(8,128)(2,1)} %constant.11.clone.inv_hbm, f32[2,32,128]{2,1,0:T(8,128)} %constant.12.clone.twd_hbm), custom_call_target="tpu_custom_call" | custom-call | flops 2000000000 | bytes 2097152 | tf_op jit(solution)/shard_map/compress/pallas_call | solution.py:243
  3.8 0.0 copy-start.2
  3.8 144.5 %all_to_all.15.x_ref = f32[32,64,128]{2,1,0:T(8,128)S(1)} all-to-all(f32[32,64,128]{2,1,0:T(8,128)S(1)} %compress.1), channel_id=1, replica_groups={{0,8,248,16,48,56,40,96,32,104,80,112,120,72,88,192,64,200,216,208,240,..., dimensions={0} | all-to-all | bytes 2097152 | tf_op jit(solution)/shard_map/all_to_all | solution.py:498
  148.3 0.0 copy-done.2
  148.3 1.0 doppler.1
  149.3 0.0 copy-start.1
  149.3 0.0 copy-start
  149.3 5.8 %collective-permute-start = (f32[256,128]{1,0:T(8,128)S(1)}, f32[256,128]{1,0:T(8,128)S(1)}, u32[]{:S(2)}, u32[]{:S(2)}) collective-permute-start(f32[256,128]{1,0:T(8,128)S(1)} %get-tuple-element.17), channel_id=1, source_target_pairs={{0,8},{8,0},{16,24},{24,16},{32,40},{40,32},{48,56},{56,48},{64,72... | collective-permute-start | bytes 393224 | tf_op jit(solution)/shard_map/ppermute | solution.py:502
  155.1 0.7 collective-permute-start.1
  155.8 0.0 copy-done.1
  155.8 0.0 copy-done
  155.8 0.7 windows.1
  156.5 0.3 core.1.noise_ref
  156.9 1.2 collective-permute-done.first_ref
  158.1 0.0 collective-permute-done.1.second_ref
  158.1 1.2 cfar.1
  159.2 7.7 %all_to_all.16 = f32[8,1,128]{2,1,0:T(1,128)S(1)} all-to-all(f32[8,1,128]{2,1,0:T(1,128)S(1)} %bitcast.10), channel_id=1, replica_groups={{5,4,7,6,1,0,3,2},{13,12,15,14,9,8,11,10},{21,20,23,22,17,16,19,18},{29..., dimensions={0} | all-to-all | bytes 8192 | tf_op jit(solution)/shard_map/all_to_all | solution.py:510
  167.0 27.0 %all_to_all.17 = f32[32,1,128]{2,1,0:T(1,128)S(1)} all-to-all(f32[32,1,128]{2,1,0:T(1,128)S(1)} %broadcast_in_dim.2), channel_id=1, replica_groups={{128,136,144,152,160,168,176,184,192,200,208,216,224,232,240,248,0,8,16..., dimensions={0} | all-to-all | bytes 32768 | tf_op jit(solution)/shard_map/all_to_all | solution.py:511
  194.0 0.6 finish.1
  (2 shorter events, 0.0 us)
Async XLA Ops:
  3.8 144.5 %copy-start.2 = (bf16[4,2,256,256]{3,2,1,0:T(8,128)(2,1)S(1)}, bf16[4,2,256,256]{3,2,1,0:T(8,128)(2,1)}, u32[]{:S(2)}) copy-start(bf16[4,2,256,256]{3,2,1,0:T(8,128)(2,1)} %constant.13.clone.tab_ref) | copy-start | bytes 3145732
  149.3 6.5 %copy-start.1 = (s32[2,2]{1,0:T(2,128)S(1)}, s32[2,2]{1,0:T(2,128)}, u32[]{:S(2)}) copy-start(s32[2,2]{1,0:T(2,128)} %thresh_ref.1) | copy-start | bytes 52
  149.3 6.5 %copy-start = (s32[2,2]{1,0:T(2,128)S(1)}, s32[2,2]{1,0:T(2,128)}, u32[]{:S(2)}) copy-start(s32[2,2]{1,0:T(2,128)} %window_ref) | copy-start | bytes 52
  149.3 8.7 %collective-permute-start = (f32[256,128]{1,0:T(8,128)S(1)}, f32[256,128]{1,0:T(8,128)S(1)}, u32[]{:S(2)}, u32[]{:S(2)}) collective-permute-start(f32[256,128]{1,0:T(8,128)S(1)} %get-tuple-element.17), channel_id=1, source_target_pairs={{0,8},{8,0},{16,24},{24,16},{32,40},{40,32},{48,56},{56,48},{64,72... | collective-permute-start | bytes 393224 | tf_op jit(solution)/shard_map/ppermute | solution.py:502
  155.1 2.9 %collective-permute-start.1 = (f32[256,128]{1,0:T(8,128)S(1)}, f32[256,128]{1,0:T(8,128)S(1)}, u32[]{:S(2)}, u32[]{:S(2)}) collective-permute-start(f32[256,128]{1,0:T(8,128)S(1)} %get-tuple-element.18), channel_id=1, source_target_pairs={{8,16},{16,8},{24,32},{32,24},{40,48},{48,40},{56,64},{64,56},{72,... | collective-permute-start | bytes 393224 | tf_op jit(solution)/shard_map/ppermute | solution.py:503

commit v7 on v6

--- a/solution.py
+++ b/solution.py
@@ -162,7 +162,7 @@
     load_twd = pltpu.make_async_copy(twd_hbm, twd_ref, sems.at[n + 1])
     load_fwd = pltpu.make_async_copy(fwd_hbm, fwd_ref, sems.at[n + 2])
     load_inv = pltpu.make_async_copy(inv_hbm, inv_ref, sems.at[n + 3])
-    for load in [loads[0], load_rep, load_twd, load_fwd, *loads[1:], load_inv]:
+    for load in [load_rep, loads[0], load_twd, *loads[1:], load_fwd, load_inv]:
         load.start()
 
     load_rep.wait()

time: 195 us -> 195 us (level)
  no operation moved by 1% of the time
where the time goes in v7:
time: 195 us
  blocking collectives  179 us (92%)
  Pallas kernels  6.96 us (4%)
  starting transfers between devices  6.43 us (3%)
    all_to_all x1, blocking collectives, local(): received = lax.all_to_all(ready, 'pulse', 0, 0, axis_index_groups=[ORDER])  144 us
    all_to_all x1, blocking collectives, local(): lax.all_to_all(jnp.broadcast_to(plane, (groups, 1, LANES)), 'pulse', 0, 0...  27 us
    all_to_all x1, blocking collectives, local(): lax.all_to_all(soft, ('chan', 'sub'), 0, 0, axis_index_groups=[near])  7.73 us
    ppermute x1, starting transfers between devices, local(): first = lax.ppermute(first, 'pulse', [(i, i ^ 1) for i in range(groups)])  5.76 us
  transfers between devices with their start and end apart: 2, of which 1 were waited for; matrix products, arithmetic and copies ran while one was open for 0% of the time, Pallas kernels for 1%

profile of v7, /device:TPU:40, one launch (start us, length us, event | category | flops | bytes accessed | tf_op | source)
XLA Modules:
  0.0 194.6 jit_solution(1778432987877002327)
XLA Ops:
  0.6 3.1 %compress.1 = f32[32,64,128]{2,1,0:T(8,128)S(1)} custom-call(s32[2,2,16,4096]{3,2,1,0:T(8,128)} %x_hbm.1, f32[64,128]{1,0:T(8,128)} %bitcast.11, bf16[2,256,256]{2,1,0:T(8,128)(2,1)} %constant.10.clone.fwd_hbm, bf16[2,256,256]{2,1,0:T(8,128)(2,1)} %constant.11.clone.inv_hbm, f32[2,32,128]{2,1,0:T(8,128)} %constant.12.clone.twd_hbm), custom_call_target="tpu_custom_call" | custom-call | flops 2000000000 | bytes 2097152 | tf_op jit(solution)/shard_map/compress/pallas_call | solution.py:243
  3.7 0.0 copy-start.2
  3.7 144.5 %all_to_all.15.x_ref = f32[32,64,128]{2,1,0:T(8,128)S(1)} all-to-all(f32[32,64,128]{2,1,0:T(8,128)S(1)} %compress.1), channel_id=1, replica_groups={{0,8,248,16,48,56,40,96,32,104,80,112,120,72,88,192,64,200,216,208,240,..., dimensions={0} | all-to-all | bytes 2097152 | tf_op jit(solution)/shard_map/all_to_all | solution.py:498
  148.2 0.0 copy-done.2
  148.2 1.0 doppler.1
  149.3 0.0 copy-start.1
  149.3 0.0 copy-start
  149.3 5.8 %collective-permute-start = (f32[256,128]{1,0:T(8,128)S(1)}, f32[256,128]{1,0:T(8,128)S(1)}, u32[]{:S(2)}, u32[]{:S(2)}) collective-permute-start(f32[256,128]{1,0:T(8,128)S(1)} %get-tuple-element.17), channel_id=1, source_target_pairs={{0,8},{8,0},{16,24},{24,16},{32,40},{40,32},{48,56},{56,48},{64,72... | collective-permute-start | bytes 393224 | tf_op jit(solution)/shard_map/ppermute | solution.py:502
  155.1 0.7 collective-permute-start.1
  155.7 0.0 copy-done.1
  155.7 0.0 copy-done
  155.7 0.7 windows.1
  156.5 0.3 core.1.noise_ref
  156.8 1.2 collective-permute-done.first_ref
  158.0 0.0 collective-permute-done.1.second_ref
  158.0 1.2 cfar.1
  159.2 7.7 %all_to_all.16 = f32[8,1,128]{2,1,0:T(1,128)S(1)} all-to-all(f32[8,1,128]{2,1,0:T(1,128)S(1)} %bitcast.10), channel_id=1, replica_groups={{5,4,7,6,1,0,3,2},{13,12,15,14,9,8,11,10},{21,20,23,22,17,16,19,18},{29..., dimensions={0} | all-to-all | bytes 8192 | tf_op jit(solution)/shard_map/all_to_all | solution.py:510
  166.9 27.0 %all_to_all.17 = f32[32,1,128]{2,1,0:T(1,128)S(1)} all-to-all(f32[32,1,128]{2,1,0:T(1,128)S(1)} %broadcast_in_dim.2), channel_id=1, replica_groups={{128,136,144,152,160,168,176,184,192,200,208,216,224,232,240,248,0,8,16..., dimensions={0} | all-to-all | bytes 32768 | tf_op jit(solution)/shard_map/all_to_all | solution.py:511
  193.9 0.6 finish.1
  (2 shorter events, 0.0 us)
Async XLA Ops:
  3.7 144.5 %copy-start.2 = (bf16[4,2,256,256]{3,2,1,0:T(8,128)(2,1)S(1)}, bf16[4,2,256,256]{3,2,1,0:T(8,128)(2,1)}, u32[]{:S(2)}) copy-start(bf16[4,2,256,256]{3,2,1,0:T(8,128)(2,1)} %constant.13.clone.tab_ref) | copy-start | bytes 3145732
  149.3 6.5 %copy-start.1 = (s32[2,2]{1,0:T(2,128)S(1)}, s32[2,2]{1,0:T(2,128)}, u32[]{:S(2)}) copy-start(s32[2,2]{1,0:T(2,128)} %thresh_ref.1) | copy-start | bytes 52
  149.3 6.5 %copy-start = (s32[2,2]{1,0:T(2,128)S(1)}, s32[2,2]{1,0:T(2,128)}, u32[]{:S(2)}) copy-start(s32[2,2]{1,0:T(2,128)} %window_ref) | copy-start | bytes 52
  149.3 8.7 %collective-permute-start = (f32[256,128]{1,0:T(8,128)S(1)}, f32[256,128]{1,0:T(8,128)S(1)}, u32[]{:S(2)}, u32[]{:S(2)}) collective-permute-start(f32[256,128]{1,0:T(8,128)S(1)} %get-tuple-element.17), channel_id=1, source_target_pairs={{0,8},{8,0},{16,24},{24,16},{32,40},{40,32},{48,56},{56,48},{64,72... | collective-permute-start | bytes 393224 | tf_op jit(solution)/shard_map/ppermute | solution.py:502
  155.1 2.9 %collective-permute-start.1 = (f32[256,128]{1,0:T(8,128)S(1)}, f32[256,128]{1,0:T(8,128)S(1)}, u32[]{:S(2)}, u32[]{:S(2)}) collective-permute-start(f32[256,128]{1,0:T(8,128)S(1)} %get-tuple-element.18), channel_id=1, source_target_pairs={{8,16},{16,8},{24,32},{32,24},{40,48},{48,40},{56,64},{64,56},{72,... | collective-permute-start | bytes 393224 | tf_op jit(solution)/shard_map/ppermute | solution.py:503
